TPU v7x, 128 devices: a whole 4x4x4 slice. The times are simulated.
128 devices in a mesh: dp: 64 (over x, y, z_lo, core), section: 2 (over z_hi).
Axes of the slice: x: 4, y: 4, z: 4 (z_hi: 2, z_lo: 2; z = z_hi * 2 + z_lo), core: 2. Of those that a mesh axis runs over, the one named last changes fastest.
Arguments:
- samples: bfloat16 [512, 512], P('dp'), may hold values from -16 to 16
- targets: bfloat16 [512, 512], P('dp'), may hold values from -16 to 16
- jacobian_targets: bfloat16 [512, 128, 512], P('dp'), may hold values from -0.1796875 to 0.1796875
- directions: int32 [512, 128], P('dp'), may hold values from 0 to 511
- plan: int32 [64, 8], P('dp'), may hold values from 0 to 7, each once within a row
- weights: bfloat16 [2, 512, 8192], P('section'), may hold values from -1 to 1
Outputs:
- gradients: float32 [2, 512, 8192], P('section', 'dp')
Inputs may be any that keep to these rules, and one draw needn't show every extreme that they name: `plan`: each row is a permutation of 0 to 7.
All inputs are finite; a program needn't handle non-finite values.
Results may differ from a plain program's by a relative error of at most 0.0034.
Values may be sent and summed in bfloat16 or wider, within the bound.
A program may use at most 128 MiB of HBM per device.

v0:
```python
import jax
import jax.numpy as jnp
from jax import lax
from jax.sharding import Mesh
from jax.sharding import PartitionSpec as P

MICRO = 4
BATCH = 1
DP = ("dp_0", "dp_1", "dp_2", "dp_3")


jacobian_weight = 32.0


def partner(block, axis, distance):
    count = lax.axis_size(axis)
    route = []
    for low in range(count):
        high = low | 1 << distance
        if high != low and high < count:
            route += [(low, high), (high, low)]
    return lax.ppermute(block, axis, route)


def sent_to_all(shard, axis):
    copies = jnp.broadcast_to(shard, (lax.axis_size(axis), *shard.shape))
    return lax.all_to_all(copies, axis, split_axis=0, concat_axis=0, tiled=True)


def of_everyone(shard, axis):
    return sent_to_all(shard, axis).sum(axis=0)


def packed_total(arrays, axis):
    ends = [0]
    for a in arrays:
        ends.append(ends[-1] + a.size)
    subtotal = of_everyone(jnp.concatenate([a.ravel() for a in arrays]), axis)
    return tuple((subtotal[b:e].reshape(a.shape) for a, b, e in zip(arrays, ends, ends[1:])))


def cut_along(shard, dim, length):
    before, after = (shard.shape[:dim], shard.shape[dim + 1 :])
    return jnp.moveaxis(shard.reshape(*before, length, -1, *after), dim, 0)


def scatter_pairs(shard, chips, core, dim):
    sizes = (lax.axis_size(chips), lax.axis_size(core))
    tiles = cut_along(shard, dim, sizes[0] * sizes[1])
    inside = tiles.shape[1:]
    tiles = tiles.reshape(*sizes, *inside).swapaxes(0, 1).reshape(-1, *inside)
    tiles = lax.psum_scatter(tiles, core, scatter_dimension=0, tiled=True)
    return lax.psum_scatter(tiles, chips, scatter_dimension=0, tiled=True)[0]


def contract_rows(left, right):
    return lax.dot_general(
        left, right, (((0,), (0,)), ((), ())), preferred_element_type=jnp.float32
    )


def against_rows(left, right):
    return lax.dot_general(
        left, right, (((1,), (1,)), ((), ())), preferred_element_type=jnp.float32
    )


def encoder_parts(inputs, chosen_dirs, w_first):
    linear = jnp.dot(inputs, w_first, preferred_element_type=jnp.float32)
    squash = jax.nn.sigmoid(linear)
    first_slope = squash * (1.0 + linear * (1.0 - squash))
    second_slope = squash * (1.0 - squash) * (2.0 + linear * (1.0 - 2.0 * squash))
    picked = jnp.take(w_first, chosen_dirs, axis=0)
    return (linear, squash, first_slope, second_slope, picked)


def encoder_forward(encoded):
    linear, squash, first_slope, second_slope, picked = encoded
    hidden = (linear * squash).astype(jnp.bfloat16)
    tangent = (first_slope[:, None, :] * picked.astype(jnp.float32)).astype(jnp.bfloat16)
    return (hidden, tangent)


def encoder_backward(inputs, chosen_dirs, encoded, cotangent, cotangent_tangent, reduced):
    linear, squash, first_slope, second_slope, picked = encoded
    projected = jnp.sum(cotangent_tangent.astype(jnp.float32) * picked.astype(jnp.float32), axis=1)
    grad_pre = (cotangent.astype(jnp.float32) * first_slope + second_slope * projected).astype(
        jnp.bfloat16
    )
    grad_picked = (cotangent_tangent.astype(jnp.float32) * first_slope[:, None, :]).astype(
        jnp.bfloat16
    )
    columns = grad_pre.shape[1]
    onehot = (
        chosen_dirs.reshape(-1)[:, None] == jnp.arange(reduced, dtype=jnp.int32)[None, :]
    ).astype(jnp.bfloat16)
    return contract_rows(inputs, grad_pre) + contract_rows(onehot, grad_picked.reshape(-1, columns))


def shards(samples, targets, jacobian_targets, directions, plan, weights):
    section_index = lax.axis_index("section")
    weight = weights[0]
    reduced, columns = weight.shape
    order_row = plan[0]

    def batch_slots(micro_index):
        return lax.dynamic_slice_in_dim(order_row, micro_index * BATCH, BATCH)

    def encoder_rows(micro_index):
        chosen = batch_slots(micro_index)
        return (jnp.take(samples, chosen, axis=0), jnp.take(directions, chosen, axis=0))

    def decoder_rows(micro_index):
        chosen = batch_slots(micro_index)
        return (jnp.take(targets, chosen, axis=0), jnp.take(jacobian_targets, chosen, axis=0))

    half = columns // 2
    keep_part = lax.dynamic_slice_in_dim(weight, section_index * half, half, 1)
    give_part = lax.dynamic_slice_in_dim(weight, (1 - section_index) * half, half, 1)
    other_part = partner(give_part, "section", 0)
    w_first, w_last = lax.cond(
        section_index == 0, lambda: (keep_part, other_part), lambda: (other_part, keep_part)
    )
    cleared_half = jnp.zeros((reduced, half), jnp.float32)

    def advance(current, carried):
        first_total, last_total = carried
        inputs, chosen_dirs = encoder_rows(current)
        target_rows, jacobian_rows = decoder_rows(current)
        encoded = encoder_parts(inputs, chosen_dirs, w_first)
        hidden, tangent = encoder_forward(encoded)
        flattened = tangent.reshape(-1, half)
        output, jacobian = packed_total(
            (against_rows(hidden, w_last), against_rows(flattened, w_last)), "section"
        )
        misfit = (output - target_rows.astype(jnp.float32)).astype(jnp.bfloat16)
        jac_misfit = (
            jacobian_weight * (jacobian - jacobian_rows.reshape(jacobian.shape).astype(jnp.float32))
        ).astype(jnp.bfloat16)
        grad_last = contract_rows(misfit, hidden) + contract_rows(jac_misfit, flattened)
        cotangent = jnp.dot(misfit, w_last, preferred_element_type=jnp.float32).astype(jnp.bfloat16)
        cotangent_tangent = jnp.dot(jac_misfit, w_last, preferred_element_type=jnp.float32).astype(
            jnp.bfloat16
        )
        cotangent_tangent = cotangent_tangent.reshape(tangent.shape)
        grad_first = encoder_backward(
            inputs, chosen_dirs, encoded, cotangent, cotangent_tangent, reduced
        )
        return (first_total + grad_first, last_total + grad_last)

    first_total, last_total = lax.fori_loop(0, MICRO, advance, (cleared_half, cleared_half))
    stacked = jnp.stack([first_total, last_total])
    row_sums = scatter_pairs(stacked, ("dp_0", "dp_1", "dp_2"), "dp_3", 1)
    result = lax.all_to_all(row_sums, "section", split_axis=0, concat_axis=2, tiled=True)
    return result


def solution(mesh):
    torus = Mesh(
        mesh.devices.reshape(4, 4, 2, 2, mesh.shape["section"]),
        ("dp_0", "dp_1", "dp_2", "dp_3", "section"),
    )
    return jax.shard_map(
        shards,
        mesh=torus,
        in_specs=(
            P(DP, None),
            P(DP, None),
            P(DP, None, None),
            P(DP, None),
            P(DP, None),
            P("section", None, None),
        ),
        out_specs=P("section", DP, None),
        check_vma=False,
    )
```

profile of v0, /device:TPU:1, one launch (start us, length us, event | category | flops | bytes accessed | tf_op | source)
XLA Modules:
  0.0 571.4 jit_solution(5117243101292586576)
XLA Ops:
  6.5 7.8 %dynamic-slice_bitcast_fusion = (bf16[512,4096]{1,0:T(8,128)(2,1)}, bf16[512,4096]{1,0:T(8,128)(2,1)}) fusion(bf16[1,512,8192]{2,1,0:T(8,128)(2,1)} %param.17, s32[]{:T(128)S(6)} %select_n.137, s32[]{:T(128)S(6)} %select_n.136), kind=kLoop, calls=%fused_computation.49 | loop fusion | bytes 16777224 | tf_op jit(solution)/shard_map/dynamic_slice | solution.py:118
  14.4 4.4 collective-permute-start
  18.8 90.6 %collective-permute-done = bf16[512,4096]{1,0:T(8,128)(2,1)} collective-permute-done((bf16[512,4096]{1,0:T(8,128)(2,1)}, bf16[512,4096]{1,0:T(8,128)(2,1)}, u32[]{:S(2)}, u32[]{:S(2)}) %collective-permute-start) | collective-permute-done | bytes 4194336 | tf_op jit(solution)/shard_map/ppermute | solution.py:22
  109.4 6.9 %conditional.1 = (bf16[512,4096]{1,0:T(8,128)(2,1)S(1)}, bf16[512,4096]{1,0:T(8,128)(2,1)}) conditional(s32[]{:T(128)} %convert_element_type.116, (bf16[512,4096]{1,0:T(8,128)(2,1)}, bf16[512,4096]{1,0:T(8,128)(2,1)}) %tuple.26, (bf16[512,4096]{1,0:T(8,128)(2,1)}, bf16[512,4096]{1,0:T(8,128)(2,1)}) %tuple.27), branch_computations={%region_0.0_spmd, %region_1.0_spmd} | conditional | bytes 16777232 | solution.py:121
  109.4 2.2 copy.19
  111.6 4.7 copy.20
  116.3 1.9 copy-done.2
  118.2 200.7 %while.19 = (s32[]{:T(128)}, f32[512,4096]{1,0:T(8,128)}, f32[512,4096]{1,0:T(8,128)}, s32[8]{0:T(128)S(1)}, bf16[8,512]{1,0:T(8,128)(2,1)S(1)}, /*index=5*/bf16...) while((s32[]{:T(128)}, f32[512,4096]{1,0:T(8,128)}, ...), condition=%wide.region_5.7_spmd.clone, body=%wide.region_2.6_spmd.clone.sunk | while | flops 2186210560 | bytes 104153424 | solution.py:151
  121.5 2.8 fusion.70
  124.4 4.9 gather_fusion
  129.3 3.5 fusion.72
  135.6 3.5 all-to-all-start
  139.1 8.3 %all-to-all-done = f32[2,1,66048]{2,1,0:T(1,128)S(1)} async-done(((f32[2,1,66048]{2,1,0:T(1,128)}), f32[2,1,66048]{2,1,0:T(1,128)S(1)}, u32[]{:S(2)}, u32[]{:S(2)}) %all-to-all-start) | async-done | bytes 528416 | tf_op jit(solution)/shard_map/while/body/eval_jaxpr/all_to_all | solution.py:27
  149.2 3.1 fusion.75
  152.2 1.8 fusion.73
  154.1 5.8 %select_add_fusion.5 = f32[512,4096]{1,0:T(8,128)} fusion(f32[512,4096]{1,0:T(8,128)} %get-tuple-element.391, f32[4096]{0:T(1024)S(1)} %get-tuple-element.367, f32[512]{0:T(512)S(1)} %convert.45, pred[]{:T(512)S(6)} %compare.6, f32[4096]{0:T(1024)S(1)} %get-tuple-element.361, bf16[128,4096]{1,0:T(8,128)(2,1)S(1)} %gather_fusion, ...), kind=kOutput, calls=%fused_computation.1.clone.1 | convolution fusion | flops 547684352 | bytes 18254976 | tf_op jit(solution)/shard_map/while/body/eval_jaxpr/dot_general | solution.py:57
  159.9 4.9 select_add_fusion.4
  168.1 2.8 fusion.70
  171.0 4.9 gather_fusion
  175.9 3.5 fusion.72
  182.2 3.5 all-to-all-start
  185.7 7.5 %all-to-all-done = f32[2,1,66048]{2,1,0:T(1,128)S(1)} async-done(((f32[2,1,66048]{2,1,0:T(1,128)}), f32[2,1,66048]{2,1,0:T(1,128)S(1)}, u32[]{:S(2)}, u32[]{:S(2)}) %all-to-all-start) | async-done | bytes 528416 | tf_op jit(solution)/shard_map/while/body/eval_jaxpr/all_to_all | solution.py:27
  195.0 3.1 fusion.75
  198.0 1.8 fusion.73
  199.9 8.3 %select_add_fusion.5 = f32[512,4096]{1,0:T(8,128)} fusion(f32[512,4096]{1,0:T(8,128)} %get-tuple-element.391, f32[4096]{0:T(1024)S(1)} %get-tuple-element.367, f32[512]{0:T(512)S(1)} %convert.45, pred[]{:T(512)S(6)} %compare.6, f32[4096]{0:T(1024)S(1)} %get-tuple-element.361, bf16[128,4096]{1,0:T(8,128)(2,1)S(1)} %gather_fusion, ...), kind=kOutput, calls=%fused_computation.1.clone.1 | convolution fusion | flops 547684352 | bytes 18254976 | tf_op jit(solution)/shard_map/while/body/eval_jaxpr/dot_general | solution.py:57
  208.2 8.3 %select_add_fusion.4 = f32[512,4096]{1,0:T(8,128)} fusion(f32[512,4096]{1,0:T(8,128)} %get-tuple-element.390, f32[4096]{0:T(1024)S(1)} %fusion.76, f32[512]{0:T(512)S(1)} %convert.44, pred[]{:T(512)S(6)} %compare.6, f32[128,4096]{1,0:T(8,128)S(1)} %get-tuple-element.366, f32[4096]{0:T(1024)S(1)} %get-tuple-element.361, s32[128]{0:T(128)S(1)} %bitcast.110), kind=kOutput, calls=%fused_computation.2.clone.1 | convolution fusion | flops 546373632 | bytes 18909696 | tf_op jit(solution)/shard_map/while/body/eval_jaxpr/dot_general | solution.py:57
  219.8 2.8 fusion.70
  222.7 4.9 gather_fusion
  227.7 3.5 fusion.72
  233.9 3.5 all-to-all-start
  237.4 6.9 %all-to-all-done = f32[2,1,66048]{2,1,0:T(1,128)S(1)} async-done(((f32[2,1,66048]{2,1,0:T(1,128)}), f32[2,1,66048]{2,1,0:T(1,128)S(1)}, u32[]{:S(2)}, u32[]{:S(2)}) %all-to-all-start) | async-done | bytes 528416 | tf_op jit(solution)/shard_map/while/body/eval_jaxpr/all_to_all | solution.py:27
  246.1 3.1 fusion.75
  251.0 8.3 %select_add_fusion.5 = f32[512,4096]{1,0:T(8,128)} fusion(f32[512,4096]{1,0:T(8,128)} %get-tuple-element.391, f32[4096]{0:T(1024)S(1)} %get-tuple-element.367, f32[512]{0:T(512)S(1)} %convert.45, pred[]{:T(512)S(6)} %compare.6, f32[4096]{0:T(1024)S(1)} %get-tuple-element.361, bf16[128,4096]{1,0:T(8,128)(2,1)S(1)} %gather_fusion, ...), kind=kOutput, calls=%fused_computation.1.clone.1 | convolution fusion | flops 547684352 | bytes 18254976 | tf_op jit(solution)/shard_map/while/body/eval_jaxpr/dot_general | solution.py:57
  259.4 8.3 %select_add_fusion.4 = f32[512,4096]{1,0:T(8,128)} fusion(f32[512,4096]{1,0:T(8,128)} %get-tuple-element.390, f32[4096]{0:T(1024)S(1)} %fusion.76, f32[512]{0:T(512)S(1)} %convert.44, pred[]{:T(512)S(6)} %compare.6, f32[128,4096]{1,0:T(8,128)S(1)} %get-tuple-element.366, f32[4096]{0:T(1024)S(1)} %get-tuple-element.361, s32[128]{0:T(128)S(1)} %bitcast.110), kind=kOutput, calls=%fused_computation.2.clone.1 | convolution fusion | flops 546373632 | bytes 18909696 | tf_op jit(solution)/shard_map/while/body/eval_jaxpr/dot_general | solution.py:57
  271.0 2.8 fusion.70
  273.9 4.9 gather_fusion
  278.8 3.5 fusion.72
  285.1 3.5 all-to-all-start
  288.6 6.9 %all-to-all-done = f32[2,1,66048]{2,1,0:T(1,128)S(1)} async-done(((f32[2,1,66048]{2,1,0:T(1,128)}), f32[2,1,66048]{2,1,0:T(1,128)S(1)}, u32[]{:S(2)}, u32[]{:S(2)}) %all-to-all-start) | async-done | bytes 528416 | tf_op jit(solution)/shard_map/while/body/eval_jaxpr/all_to_all | solution.py:27
  297.3 3.1 fusion.75
  300.3 1.8 fusion.73
  302.2 8.3 %select_add_fusion.5 = f32[512,4096]{1,0:T(8,128)} fusion(f32[512,4096]{1,0:T(8,128)} %get-tuple-element.391, f32[4096]{0:T(1024)S(1)} %get-tuple-element.367, f32[512]{0:T(512)S(1)} %convert.45, pred[]{:T(512)S(6)} %compare.6, f32[4096]{0:T(1024)S(1)} %get-tuple-element.361, bf16[128,4096]{1,0:T(8,128)(2,1)S(1)} %gather_fusion, ...), kind=kOutput, calls=%fused_computation.1.clone.1 | convolution fusion | flops 547684352 | bytes 18254976 | tf_op jit(solution)/shard_map/while/body/eval_jaxpr/dot_general | solution.py:57
  310.6 8.3 %select_add_fusion.4 = f32[512,4096]{1,0:T(8,128)} fusion(f32[512,4096]{1,0:T(8,128)} %get-tuple-element.390, f32[4096]{0:T(1024)S(1)} %fusion.76, f32[512]{0:T(512)S(1)} %convert.44, pred[]{:T(512)S(6)} %compare.6, f32[128,4096]{1,0:T(8,128)S(1)} %get-tuple-element.366, f32[4096]{0:T(1024)S(1)} %get-tuple-element.361, s32[128]{0:T(128)S(1)} %bitcast.110), kind=kOutput, calls=%fused_computation.2.clone.1 | convolution fusion | flops 546373632 | bytes 18909696 | tf_op jit(solution)/shard_map/while/body/eval_jaxpr/dot_general | solution.py:57
  318.9 6.6 %pad_maximum_fusion.1 = f32[2,64,8,4096]{3,2,1,0:T(8,128)S(1)} fusion(f32[1,64,8,4096]{3,2,1,0:T(8,128)} %bitcast.99, f32[1,64,8,4096]{3,2,1,0:T(8,128)} %bitcast.3), kind=kLoop, calls=%fused_computation.48 | loop fusion | flops 4194304 | bytes 33554432 | tf_op jit(solution)/shard_map/stack | solution.py:152
  325.5 6.0 %copy.10 = f32[32,2,2,8,4096]{4,3,2,0,1:T(8,128)} copy(f32[32,2,2,8,4096]{4,3,1,0,2:T(8,128)S(1)} %bitcast.101) | data formatting | bytes 33554432 | tf_op jit(solution)/shard_map/reshape | solution.py:51
  331.6 31.9 %reduce-scatter.3.cloned.1.call-done = f32[32,2,8,4096]{3,2,1,0:T(8,128)} async-done(((f32[64,2,8,4096]{3,2,1,0:T(8,128)}), f32[32,2,8,4096]{3,2,1,0:T(8,128)}) %reduce-scatter.3.cloned.1.call-update) | async-done | bytes 8388624 | tf_op jit(solution)/shard_map/reduce_scatter | solution.py:52
  363.5 191.4 %reduce-scatter.5.cloned.1.call-done = f32[1,2,8,4096]{3,2,1,0:T(8,128)} async-done(((f32[32,2,8,4096]{3,2,1,0:T(8,128)}), f32[1,2,8,4096]{3,2,1,0:T(8,128)}) %reduce-scatter.5.cloned.1.call-update) | async-done | bytes 262160 | tf_op jit(solution)/shard_map/reduce_scatter | solution.py:53
  554.9 9.0 %all_to_all.30 = f32[2,8,4096]{2,1,0:T(8,128)S(1)} all-to-all(f32[2,8,4096]{2,1,0:T(8,128)} %bitcast.107), channel_id=1, replica_groups=mesh['dp_0'=4,'dp_1'=4,'dp_2'=2,'dp_3'=2,'section'=2] {'section'}, dimensions={0} | all-to-all | bytes 524288 | tf_op jit(solution)/shard_map/all_to_all | solution.py:154
  (101 shorter events, 25.8 us)
Async XLA Ops:
  6.5 357.0 %reduce-scatter.3.cloned.1.call-start = ((), (), s32[]{:S(2)}) async-start(), calls=%async_computation.4 | async-start | bytes 25165824 | tf_op jit(solution)/shard_map/reduce_scatter | solution.py:52
  14.4 95.0 %collective-permute-start = (bf16[512,4096]{1,0:T(8,128)(2,1)}, bf16[512,4096]{1,0:T(8,128)(2,1)}, u32[]{:S(2)}, u32[]{:S(2)}) collective-permute-start(bf16[512,4096]{1,0:T(8,128)(2,1)} %get-tuple-element.287), channel_id=1, source_target_pairs={{0,1},{1,0},{2,3},{3,2},{4,5},{5,4},{6,7},{7,6},{8,9},{9,8},{10,11... | collective-permute-start | bytes 12582920 | tf_op jit(solution)/shard_map/ppermute | solution.py:22
  109.4 8.8 %copy-start.3 = (bf16[8,512]{1,0:T(8,128)(2,1)S(1)}, bf16[8,512]{1,0:T(8,128)(2,1)}, u32[]{:S(2)}) copy-start(bf16[8,512]{1,0:T(8,128)(2,1)} %param.12) | copy-start | bytes 24580
  109.4 8.8 %copy-start.4 = (s32[1,8]{1,0:T(1,128)S(1)}, s32[1,8]{1,0:T(1,128)}, u32[]{:S(2)}) copy-start(s32[1,8]{1,0:T(1,128)} %param.16) | copy-start | bytes 100
  116.3 1.9 copy-start.2
  129.3 3.5 copy-start
  135.6 11.9 %all-to-all-start = ((f32[2,1,66048]{2,1,0:T(1,128)}), f32[2,1,66048]{2,1,0:T(1,128)S(1)}, u32[]{:S(2)}, u32[]{:S(2)}) async-start(f32[2,1,66048]{2,1,0:T(1,128)} %broadcast_in_dim.163), calls=%async_computation | async-start | bytes 1056768 | tf_op jit(solution)/shard_map/while/body/eval_jaxpr/all_to_all | solution.py:27
  148.3 4.0 copy-start.1
  175.9 3.5 copy-start
  182.2 11.0 %all-to-all-start = ((f32[2,1,66048]{2,1,0:T(1,128)}), f32[2,1,66048]{2,1,0:T(1,128)S(1)}, u32[]{:S(2)}, u32[]{:S(2)}) async-start(f32[2,1,66048]{2,1,0:T(1,128)} %broadcast_in_dim.163), calls=%async_computation | async-start | bytes 1056768 | tf_op jit(solution)/shard_map/while/body/eval_jaxpr/all_to_all | solution.py:27
  194.1 4.0 copy-start.1
  227.6 3.5 copy-start
  233.9 10.4 %all-to-all-start = ((f32[2,1,66048]{2,1,0:T(1,128)}), f32[2,1,66048]{2,1,0:T(1,128)S(1)}, u32[]{:S(2)}, u32[]{:S(2)}) async-start(f32[2,1,66048]{2,1,0:T(1,128)} %broadcast_in_dim.163), calls=%async_computation | async-start | bytes 1056768 | tf_op jit(solution)/shard_map/while/body/eval_jaxpr/all_to_all | solution.py:27
  245.2 4.0 copy-start.1
  278.8 3.5 copy-start
  285.1 10.4 %all-to-all-start = ((f32[2,1,66048]{2,1,0:T(1,128)}), f32[2,1,66048]{2,1,0:T(1,128)S(1)}, u32[]{:S(2)}, u32[]{:S(2)}) async-start(f32[2,1,66048]{2,1,0:T(1,128)} %broadcast_in_dim.163), calls=%async_computation | async-start | bytes 1056768 | tf_op jit(solution)/shard_map/while/body/eval_jaxpr/all_to_all | solution.py:27
  296.4 4.0 copy-start.1
  331.5 223.4 %reduce-scatter.5.cloned.1.call-start = ((), (), s32[]{:S(2)}) async-start(), calls=%async_computation.5 | async-start | bytes 8650752 | tf_op jit(solution)/shard_map/reduce_scatter | solution.py:53
Sparse Core Ops, SparseCore 0:
  331.6 31.8 reduce-scatter.2
  365.9 188.9 reduce-scatter.4
where the time goes:
time: 575 us; the launch traced here: 571 us
  waiting for transfers between devices  344 us (60%)
  matrix products  112 us (19%)
  local copies, waits for them, and re-layouts  50.5 us (9%)
  starting transfers between devices  18.4 us (3%)
  other arithmetic  16.2 us (3%)
  between operations  13.4 us (2%)
  blocking collectives  8.96 us (2%)
  loops' own time  8.37 us (1%)
    reduce_scatter x1, waiting for transfers between devices, scatter_pairs(): return lax.psum_scatter(tiles, chips, scatter_dimension=0, tiled=True)[0]  191 us
    ppermute x1, waiting for transfers between devices, partner(): return lax.ppermute(block, axis, route)  90.6 us
    dot_general x8, matrix products, contract_rows(): lax.dot_general(left, right, (((0,), (0,)), ((), ())), preferred_element_...  60.7 us
    reduce_scatter x1, waiting for transfers between devices, scatter_pairs(): tiles = lax.psum_scatter(tiles, core, scatter_dimension=0, tiled=True)  31.9 us
    all_to_all x4, waiting for transfers between devices, sent_to_all(): return lax.all_to_all(copies, axis, split_axis=0, concat_axis=0, tiled=True)  29.7 us
    dot_general x8, matrix products, against_rows(): lax.dot_general(left, right, (((1,), (1,)), ((), ())), preferred_element_...  20.3 us
    gather x4, local copies, waits for them, and re-layouts, encoder_parts(): picked = jnp.take(w_first, chosen_dirs, axis=0)  19.7 us
    all_to_all x4, starting transfers between devices, sent_to_all(): return lax.all_to_all(copies, axis, split_axis=0, concat_axis=0, tiled=True)  14 us
  transfers between devices with their start and end apart: 7, of which 7 were waited for; matrix products, arithmetic and copies ran while one was open for 0% of the time, Pallas kernels for 0%

commit v1 on v0

v1 whole, which is shorter than its diff:
```python
import jax
import jax.numpy as jnp
from jax import lax
from jax.experimental import pallas as pl
from jax.experimental.pallas import tpu as pltpu
from jax.sharding import Mesh
from jax.sharding import PartitionSpec as P

AXES = ("x", "y", "zl", "c", "zh")
DP = ("x", "y", "zl", "c")
F32 = jnp.float32
BF16 = jnp.bfloat16
MESH = pl.DeviceIdType.MESH

RED = 512
WIDTH = 8192
TAN = 128
MICRO = 4
POOL = 8
PART = WIDTH // 4
HALF = PART // 2
ROWS = 8 * TAN
NC = 512
JAC = 32.0


def nn(a, b):
    return lax.dot_general(a, b, (((1,), (0,)), ((), ())), preferred_element_type=F32)


def nt(a, b):
    return lax.dot_general(a, b, (((1,), (1,)), ((), ())), preferred_element_type=F32)


def kernel(
    plan,
    samples,
    dirs,
    targets,
    jt_hbm,
    w_hbm,
    out,
    wb,
    jt,
    s32,
    d32,
    t32,
    xd,
    e_buf,
    et_buf,
    xt_buf,
    p32,
    pk,
    tan,
    s1,
    s2,
    jac,
    ox,
    sa,
    fa,
    fb,
    ca,
    cb,
    r1,
    r2,
    mb,
    mt,
    mxt,
    mx,
    rbuf,
    ds,
    dr,
    g32,
    gst,
    p1r,
    a32,
    hst,
    p2r,
    fs,
    lsem,
    wss,
    wrs,
    xss,
    xrs,
    rss,
    rrs,
    ass_,
    ars,
    dss,
    drs,
    p1s,
    p1q,
    p2s,
    p2q,
    p3s,
    p3q,
):
    x = lax.axis_index("x")
    y = lax.axis_index("y")
    zl = lax.axis_index("zl")
    c = lax.axis_index("c")
    zh = lax.axis_index("zh")
    z = 2 * zh + zl

    def dev(px=x, py=y, pzl=zl, pc=c, pzh=zh):
        return (px, py, pzl, pc, pzh)

    def xpeer(o):
        return lax.rem(x + o, 4)

    def ypeer(o):
        return lax.rem(y + o, 4)

    n1 = dev(pzl=1 - zl)
    n2 = dev(pzl=1 - zl, pzh=1 - zh)
    mate = dev(pc=1 - c)
    here = dev()

    sends = []

    def send(src, dst, ssem, rsem, where):
        copy = pltpu.make_async_remote_copy(
            src_ref=src, dst_ref=dst, send_sem=ssem, recv_sem=rsem, device_id=where, device_id_type=MESH
        )
        copy.start()
        sends.append(copy)

    def arrived(dst, rsem):
        pltpu.make_async_remote_copy(
            src_ref=dst, dst_ref=dst, send_sem=rsem, recv_sem=rsem, device_id=here, device_id_type=MESH
        ).wait_recv()

    barrier = pltpu.get_barrier_semaphore()
    peers = [n1, n2, dev(pzh=1 - zh)]
    peers += [dev(pzl=a, pc=1 - c, pzh=b) for a in range(2) for b in range(2)]
    peers += [dev(px=xpeer(o)) for o in (1, 2, 3)]
    peers += [dev(py=ypeer(o)) for o in (1, 2, 3)]
    for peer in peers:
        pl.semaphore_signal(barrier, inc=1, device_id=peer, device_id_type=MESH)

    own_w = pltpu.make_async_copy(
        w_hbm.at[0, :, pl.ds(pl.multiple_of(PART * z, PART), PART)], wb.at[zh], lsem.at[0]
    )
    own_w.start()
    own_j = pltpu.make_async_copy(jt_hbm, jt, lsem.at[1])
    own_j.start()

    s32[...] = samples[...].astype(F32)
    d32[...] = dirs[...].astype(F32)
    t32[...] = targets[...].astype(F32)
    xd[zl, MICRO:8, :] = jnp.zeros((8 - MICRO, RED + TAN), F32)
    for i in range(MICRO):
        at = plan[0, i]
        xd[zl, i : i + 1, 0:RED] = s32[pl.ds(at, 1), :]
        xd[zl, i : i + 1, RED : RED + TAN] = d32[pl.ds(at, 1), :]

    pl.semaphore_wait(barrier, len(peers))

    def col(core, kind, place):
        return pl.multiple_of(HALF * core + 512 * kind + 128 * place, 128)

    def wslice(core, kind, place, h):
        return wb.at[1 - zh, pl.ds(256 * h, 256), pl.ds(col(core, kind, place), 128)]

    mine = (x, y)
    for h in range(2):
        for kind in range(2):
            at = col(c, kind, mine[kind])
            send(
                w_hbm.at[0, pl.ds(256 * h, 256), pl.ds(pl.multiple_of(PART * (3 - z) + at, 128), 128)],
                wb.at[zh, pl.ds(256 * h, 256), pl.ds(at, 128)],
                wss.at[h, kind, 0],
                wrs.at[h, kind, 0],
                n2,
            )
    send(xd.at[zl], xd.at[zl], xss.at[0], xrs.at[0], n1)

    for h in range(2):
        for kind in range(2):
            piece = wslice(c, kind, mine[kind], h)
            arrived(piece, wrs.at[h, kind, 0])
            for o in (1, 3, 2):
                to = dev(px=xpeer(o)) if kind == 0 else dev(py=ypeer(o))
                send(piece, piece, wss.at[h, kind, o], wrs.at[h, kind, o], to)
            send(piece, piece, wss.at[h, kind, 4], wrs.at[h, kind, 4], mate)

    arrived(xd.at[1 - zl], xrs.at[0])
    for j in range(8):
        row = xd[j // 4, j % 4 : j % 4 + 1, RED : RED + TAN]
        level = lax.broadcasted_iota(jnp.int32, (RED, TAN), 0).astype(F32)
        hot = jnp.where(level == row, 1.0, 0.0)
        et_buf[:, TAN * j : TAN * (j + 1)] = hot.astype(BF16)
        e_buf[TAN * j : TAN * (j + 1), :] = jnp.transpose(hot).astype(BF16)
    x16 = jnp.concatenate([xd[0, 0:4, 0:RED], xd[1, 0:4, 0:RED], jnp.zeros((8, RED), F32)], axis=0)
    e_buf[ROWS : ROWS + 16, :] = x16.astype(BF16)
    xt_buf[...] = jnp.transpose(x16).astype(BF16)

    for h in range(2):
        for o in (1, 3, 2):
            for kind in range(2):
                piece = wslice(c, kind, lax.rem(mine[kind] + 4 - o, 4), h)
                arrived(piece, wrs.at[h, kind, o])
                send(piece, piece, wss.at[h, kind, 4 + o], wrs.at[h, kind, 4 + o], mate)
    for h in range(2):
        for o in (0, 1, 3, 2):
            for kind in range(2):
                arrived(wslice(1 - c, kind, lax.rem(mine[kind] + 4 - o, 4), h), wrs.at[h, kind, 4 + o])
    own_w.wait()

    jac[...] = jnp.zeros_like(jac)

    @pl.loop(0, PART // NC)
    def _(n):
        cols = pl.ds(pl.multiple_of(n * NC, NC), NC)
        p32[...] = nn(e_buf[...], wb[0, :, cols])
        linear = p32[ROWS : ROWS + 8, :]
        squash = 1.0 / (1.0 + jnp.exp(-linear))
        slope = squash * (1.0 + linear * (1.0 - squash))
        s1[:, cols] = slope
        s2[:, cols] = squash * (1.0 - squash) * (2.0 + linear * (1.0 - 2.0 * squash))
        hidden = jnp.concatenate([linear * squash, jnp.zeros((8, NC), F32)], axis=0)
        tan[ROWS : ROWS + 16, cols] = hidden.astype(BF16)
        for j in range(8):
            rows = slice(TAN * j, TAN * (j + 1))
            picked = p32[rows, :]
            pk[rows, cols] = picked.astype(BF16)
            tan[rows, cols] = (slope[j : j + 1, :] * picked).astype(BF16)
        jac[...] += nt(tan[:, cols], wb[1, :, cols])

    own = 2 * zl + zh
    b1 = 2 * (1 - zl) + zh
    b2 = 2 * (1 - zl) + (1 - zh)
    bo = 2 * zl + (1 - zh)
    for b in range(4):
        o8 = jnp.concatenate([jac[ROWS + 2 * b : ROWS + 2 * b + 2, :], jnp.zeros((14, RED), F32)], axis=0)
        ox[b] = o8
        sa[b, 0:256, :] = jac[256 * b : 256 * b + 256, :].astype(BF16)
        sa[b, 256:272, :] = o8.astype(BF16)
    lo, hi = pl.ds(0, 128), pl.ds(128, 144)
    send(sa.at[bo, lo], fa, rss.at[0], rrs.at[0], n1)
    send(sa.at[bo, hi], fb, rss.at[1], rrs.at[1], n2)
    send(sa.at[b1, lo], r1.at[lo], rss.at[2], rrs.at[2], n1)
    send(sa.at[b2, hi], r2.at[hi], rss.at[3], rrs.at[3], n2)
    arrived(fa, rrs.at[0])
    ca[...] = (sa[b2, 0:128, :].astype(F32) + fa[...].astype(F32)).astype(BF16)
    send(ca, r2.at[lo], rss.at[4], rrs.at[4], n2)
    arrived(fb, rrs.at[1])
    cb[...] = (sa[b1, 128:272, :].astype(F32) + fb[...].astype(F32)).astype(BF16)
    send(cb, r1.at[hi], rss.at[5], rrs.at[5], n1)

    own_j.wait()
    arrived(r1.at[lo], rrs.at[2])
    arrived(r2.at[lo], rrs.at[4])
    p0 = plan[0, 2 * zh]
    p1 = plan[0, 2 * zh + 1]
    full = jac[pl.ds(pl.multiple_of(256 * own, 256), 128), :]
    full = full + r1[0:128, :].astype(F32) + r2[0:128, :].astype(F32)
    mb[own, 0:128, :] = (JAC * (full - jt[p0].astype(F32))).astype(BF16)
    send(mb.at[own, lo], mb.at[own, lo], ass_.at[0], ars.at[0], n1)
    send(mb.at[own, lo], mb.at[own, lo], ass_.at[1], ars.at[1], n2)
    arrived(r2.at[hi], rrs.at[3])
    arrived(r1.at[hi], rrs.at[5])
    full = jac[pl.ds(pl.multiple_of(256 * own + 128, 128), 128), :]
    full = full + r1[128:256, :].astype(F32) + r2[128:256, :].astype(F32)
    mb[own, 128:256, :] = (JAC * (full - jt[p1].astype(F32))).astype(BF16)
    full = ox[own] + r1[256:272, :].astype(F32) + r2[256:272, :].astype(F32)
    goal = jnp.concatenate([t32[pl.ds(p0, 1), :], t32[pl.ds(p1, 1), :], jnp.zeros((14, RED), F32)], axis=0)
    mb[own, 256:272, :] = (full - goal).astype(BF16)
    send(mb.at[own, hi], mb.at[own, hi], ass_.at[2], ars.at[2], n1)
    send(mb.at[own, hi], mb.at[own, hi], ass_.at[3], ars.at[3], n2)
    arrived(mb.at[b1, lo], ars.at[0])
    send(mb.at[b1, lo], mb.at[b1, lo], ass_.at[4], ars.at[4], n2)
    arrived(mb.at[b2, hi], ars.at[3])
    send(mb.at[b2, hi], mb.at[b2, hi], ass_.at[5], ars.at[5], n1)
    arrived(mb.at[b2, lo], ars.at[1])
    arrived(mb.at[b1, hi], ars.at[2])
    arrived(mb.at[bo, lo], ars.at[4])
    arrived(mb.at[bo, hi], ars.at[5])

    for b in range(4):
        mt[:, 256 * b : 256 * b + 256] = jnp.transpose(mb[b, 0:256, :])
    heads = [mb[b, 256:272, :].astype(F32)[0:2, :] for b in range(4)]
    m16 = jnp.concatenate(heads + [jnp.zeros((8, RED), F32)], axis=0)
    mx[...] = m16.astype(BF16)
    mxt[...] = jnp.transpose(m16).astype(BF16)

    def grads(start):
        cols = pl.ds(pl.multiple_of(start, NC), NC)
        last = nn(mt[...], tan[0:ROWS, cols]) + nn(mxt[...], tan[ROWS : ROWS + 16, cols])
        g32[1] = last
        w1 = wb[1, :, cols]
        for b in range(4):
            p32[256 * b : 256 * b + 256, :] = nn(mb[b, 0:256, :], w1)
        cx = nn(mx[...], w1).astype(BF16).astype(F32)
        pre = []
        for j in range(8):
            rows = slice(TAN * j, TAN * (j + 1))
            ct = p32[rows, :].astype(BF16).astype(F32)
            slope = s1[j : j + 1, cols]
            projected = jnp.sum(ct * pk[rows, cols].astype(F32), axis=0, keepdims=True)
            pre.append(cx[j : j + 1, :] * slope + s2[j : j + 1, cols] * projected)
            rbuf[rows, :] = (ct * slope).astype(BF16)
        pre16 = jnp.concatenate(pre + [jnp.zeros((8, NC), F32)], axis=0).astype(BF16)
        g32[0] = nn(et_buf[...], rbuf[...]) + nn(xt_buf[...], pre16)

    lr = 32
    for q in range(4):
        if q < 2:
            grads(HALF * (1 - c) + NC * q)
            ds[q] = g32[...].astype(BF16)
            send(ds.at[q], dr.at[q], dss.at[q], drs.at[q], mate)
            continue
        q = q - 2
        grads(HALF * c + NC * q)
        arrived(dr.at[q], drs.at[q])
        total = g32[...] + dr[q].astype(F32)
        a32[q] = total.reshape(2, 4, 4, lr, NC)
        gst[q] = total.astype(BF16).reshape(2, 4, 4, lr, NC)
        for o in (2, 1, 3):
            if q == 0:
                src, to = gst.at[q, :, xpeer(o)], dev(px=xpeer(o))
            else:
                src, to = gst.at[q, :, :, ypeer(o)], dev(py=ypeer(o))
            send(src, p1r.at[q, o - 1], p1s.at[q, o - 1], p1q.at[q, o - 1], to)

    for q in range(2):
        for o in (1, 3, 2):
            arrived(p1r.at[q, o - 1], p1q.at[q, o - 1])
        total = a32[q, :, x] if q == 0 else a32[q, :, :, y]
        for o in (1, 3, 2):
            total = total + p1r[q, o - 1].astype(F32)
        hst[q] = total.astype(BF16)
        g32[0, 256 * q : 256 * q + 256, :] = total.reshape(256, NC)
        for o in (2, 1, 3):
            if q == 0:
                src, to = hst.at[q, :, ypeer(o)], dev(py=ypeer(o))
            else:
                src, to = hst.at[q, :, xpeer(o)], dev(px=xpeer(o))
            send(src, p2r.at[q, o - 1], p2s.at[q, o - 1], p2q.at[q, o - 1], to)
    for q in range(2):
        for o in (1, 3, 2):
            arrived(p2r.at[q, o - 1], p2q.at[q, o - 1])
        keep = y if q == 0 else x
        for layer in range(2):
            total = g32[0, pl.ds(pl.multiple_of(256 * q + 128 * layer + lr * keep, lr), lr), :]
            for o in (1, 3, 2):
                total = total + p2r[q, o - 1, layer].astype(F32)
            fs[layer, :, NC * q : NC * (q + 1)] = total

    where = pl.ds(pl.multiple_of(PART * z + HALF * c, HALF), HALF)
    me = 2 * z + c
    for dzh in (1, 0):
        for dzl in (1, 0):
            for dc in (1, 0):
                if dzh + dzl + dc == 0:
                    continue
                pzh, pzl, pc = (lax.rem(a + b, 2) for a, b in ((zh, dzh), (zl, dzl), (c, dc)))
                at = pl.multiple_of(16 * pzl + 8 * pc, 8)
                k = 4 * dzh + 2 * dzl + dc - 1
                send(
                    fs.at[pzh, pl.ds(at, 8), :],
                    out.at[:, where],
                    p3s.at[k],
                    p3q.at[k],
                    dev(pzl=pzl, pc=pc, pzh=pzh),
                )
    out[:, where] = fs[zh, pl.ds(pl.multiple_of(16 * zl + 8 * c, 8), 8), :]
    for dzh in (0, 1):
        for dzl in (0, 1):
            for dc in (0, 1):
                if dzh + dzl + dc == 0:
                    continue
                pzh, pzl, pc = (lax.rem(a + b, 2) for a, b in ((zh, dzh), (zl, dzl), (c, dc)))
                k = 4 * dzh + 2 * dzl + dc - 1
                at = pl.multiple_of(PART * (2 * pzh + pzl) + HALF * pc, HALF)
                arrived(out.at[:, pl.ds(at, HALF)], p3q.at[k])
    for copy in sends:
        copy.wait_send()


def shards(samples, targets, jacobian_targets, directions, plan, weights):
    vmem = pl.BlockSpec(memory_space=pltpu.VMEM)
    anywhere = pl.BlockSpec(memory_space=pl.ANY)
    dma = pltpu.SemaphoreType.DMA
    v = pltpu.VMEM
    result = pl.pallas_call(
        kernel,
        out_shape=jax.ShapeDtypeStruct((8, WIDTH), F32),
        in_specs=[pl.BlockSpec(memory_space=pltpu.SMEM), vmem, vmem, vmem, anywhere, anywhere],
        out_specs=vmem,
        scratch_shapes=[
            v((2, RED, PART), BF16),
            v((POOL, TAN, RED), BF16),
            v((POOL, RED), F32),
            v((POOL, TAN), F32),
            v((POOL, RED), F32),
            v((2, 8, RED + TAN), F32),
            v((ROWS + 16, RED), BF16),
            v((RED, ROWS), BF16),
            v((RED, 16), BF16),
            v((ROWS + 16, NC), F32),
            v((ROWS, PART), BF16),
            v((ROWS + 16, PART), BF16),
            v((8, PART), F32),
            v((8, PART), F32),
            v((ROWS + 16, RED), F32),
            v((4, 16, RED), F32),
            v((4, 272, RED), BF16),
            v((128, RED), BF16),
            v((144, RED), BF16),
            v((128, RED), BF16),
            v((144, RED), BF16),
            v((272, RED), BF16),
            v((272, RED), BF16),
            v((4, 272, RED), BF16),
            v((RED, ROWS), BF16),
            v((RED, 16), BF16),
            v((16, RED), BF16),
            v((ROWS, NC), BF16),
            v((2, 2, RED, NC), BF16),
            v((2, 2, RED, NC), BF16),
            v((2, RED, NC), F32),
            v((2, 2, 4, 4, 32, NC), BF16),
            v((2, 3, 2, 4, 32, NC), BF16),
            v((2, 2, 4, 4, 32, NC), F32),
            v((2, 2, 4, 32, NC), BF16),
            v((2, 3, 2, 32, NC), BF16),
            v((2, 32, HALF), F32),
            dma((2,)),
            dma((2, 2, 8)),
            dma((2, 2, 8)),
            dma((1,)),
            dma((1,)),
            dma((6,)),
            dma((6,)),
            dma((6,)),
            dma((6,)),
            dma((2,)),
            dma((2,)),
            dma((2, 3)),
            dma((2, 3)),
            dma((2, 3)),
            dma((2, 3)),
            dma((7,)),
            dma((7,)),
        ],
        compiler_params=pltpu.CompilerParams(
            collective_id=0, has_side_effects=True, vmem_limit_bytes=60 * 1024 * 1024
        ),
        name="step",
    )(plan, samples, directions, targets, jacobian_targets, weights)
    return result[None]


def solution(mesh):
    torus = Mesh(mesh.devices.reshape(4, 4, 2, 2, 2), AXES)
    return jax.shard_map(
        shards,
        mesh=torus,
        in_specs=(
            P(DP, None),
            P(DP, None),
            P(DP, None, None),
            P(DP, None),
            P(DP, None),
            P("zh", None, None),
        ),
        out_specs=P("zh", DP, None),
        check_vma=False,
    )
```

time: 575 us -> 89.9 us (0.16)
  waiting for transfers between devices: 344 us -> 0 us
  matrix products: 112 us -> 0 us
  Pallas kernels: 0 us -> 88 us
  local copies, waits for them, and re-layouts: 50.5 us -> 1.67 us
  starting transfers between devices: 18.4 us -> 0 us
  other arithmetic: 16.2 us -> 0 us
  between operations: 13.4 us -> 0.01 us
  blocking collectives: 8.96 us -> 0 us
  loops' own time: 8.37 us -> 0 us
    reduce_scatter x2 -> x0, waiting for transfers between devices: 223 us -> none  [the longest x1 191 us: scatter_pairs(): return lax.psum_scatter(tiles, chips, scatter_dimension=0, tiled=True)[0]]
    dot_general x28 -> x0, matrix products: 112 us -> none  [the longest x8 60.7 us: contract_rows(): lax.dot_general(left, right, (((0,), (0,)), ((), ())), preferred_element_...]
    ppermute x1 -> x0, waiting for transfers between devices: 90.6 us -> none  [partner(): return lax.ppermute(block, axis, route)]
    pallas_call x0 -> x1, Pallas kernels: none -> 88 us  [shards(): pl.pallas_call(kernel, out_shape=jax.ShapeDtypeStruct((8, WIDTH), F32), i...]
    all_to_all x4 -> x0, waiting for transfers between devices: 29.7 us -> none  [sent_to_all(): return lax.all_to_all(copies, axis, split_axis=0, concat_axis=0, tiled=True)]
    gather x4 -> x0, local copies, waits for them, and re-layouts: 19.7 us -> none  [encoder_parts(): picked = jnp.take(w_first, chosen_dirs, axis=0)]
    all_to_all x4 -> x0, starting transfers between devices: 14 us -> none  [sent_to_all(): return lax.all_to_all(copies, axis, split_axis=0, concat_axis=0, tiled=True)]
    dynamic_slice x5 -> x0, local copies, waits for them, and re-layouts: 10.2 us -> none  [the longest x1 7.84 us: shards(): keep_part = lax.dynamic_slice_in_dim(weight, section_index * half, half, 1)]
  transfers between devices with their start and end apart: 7 -> 0, of which waited for: 7 -> 0; matrix products, arithmetic and copies ran while one was open for 0% -> 0% of each run, Pallas kernels for 0% -> 0%
where the time goes in v1:
time: 89.9 us; the launch traced here: 89.7 us
  Pallas kernels  88 us (98%)
  local copies, waits for them, and re-layouts  1.67 us (2%)
    pallas_call x1, Pallas kernels, shards(): pl.pallas_call(kernel, out_shape=jax.ShapeDtypeStruct((8, WIDTH), F32), i...  88 us

profile of v1, /device:TPU:1, one launch (start us, length us, event | category | flops | bytes accessed | tf_op | source)
XLA Modules:
  0.0 89.7 jit_solution(661145513741868117)
XLA Ops:
  0.0 88.0 %step.1 = f32[8,8192]{1,0:T(8,128)} custom-call(s32[1,8]{1,0:T(1,128)} %plan.1, bf16[8,512]{1,0:T(8,128)(2,1)} %samples.1, s32[8,128]{1,0:T(8,128)} %dirs.1, bf16[8,512]{1,0:T(8,128)(2,1)} %targets.1, bf16[8,128,512]{2,1,0:T(8,128)(2,1)} %jt_hbm.1, bf16[1,512,8192]{2,1,0:T(8,128)(2,1)} %w_hbm.1), custom_call_target="tpu_custom_call" | custom-call | tf_op jit(solution)/shard_map/step/pallas_call | solution.py:386
  88.0 1.7 %copy.8 = f32[1,8,8192]{2,1,0:T(8,128)} copy(f32[1,8,8192]{2,1,0:T(8,128)} %bitcast.1) | data formatting | bytes 524288

commit v2 on v1

--- a/solution.py
+++ b/solution.py
@@ -34,12 +34,15 @@
 
 def kernel(
     plan,
+    samples_hbm,
+    dirs_hbm,
+    targets_hbm,
+    jt_hbm,
+    w_hbm,
+    out,
     samples,
     dirs,
     targets,
-    jt_hbm,
-    w_hbm,
-    out,
     wb,
     jt,
     s32,
@@ -66,15 +69,15 @@
     mb,
     mt,
     mxt,
-    mx,
-    rbuf,
+    lm,
+    pr,
+    g,
     ds,
     dr,
-    g32,
     gst,
     p1r,
-    a32,
     hst,
+    h32,
     p2r,
     fs,
     lsem,
@@ -138,6 +141,10 @@
     for peer in peers:
         pl.semaphore_signal(barrier, inc=1, device_id=peer, device_id_type=MESH)
 
+    small = []
+    for k, (src, dst) in enumerate(((samples_hbm, samples), (dirs_hbm, dirs), (targets_hbm, targets))):
+        small.append(pltpu.make_async_copy(src, dst, lsem.at[2 + k]))
+        small[-1].start()
     own_w = pltpu.make_async_copy(
         w_hbm.at[0, :, pl.ds(pl.multiple_of(PART * z, PART), PART)], wb.at[zh], lsem.at[0]
     )
@@ -145,6 +152,8 @@
     own_j = pltpu.make_async_copy(jt_hbm, jt, lsem.at[1])
     own_j.start()
 
+    for copy in small:
+        copy.wait()
     s32[...] = samples[...].astype(F32)
     d32[...] = dirs[...].astype(F32)
     t32[...] = targets[...].astype(F32)
@@ -183,43 +192,46 @@
                 to = dev(px=xpeer(o)) if kind == 0 else dev(py=ypeer(o))
                 send(piece, piece, wss.at[h, kind, o], wrs.at[h, kind, o], to)
             send(piece, piece, wss.at[h, kind, 4], wrs.at[h, kind, 4], mate)
-
-    arrived(xd.at[1 - zl], xrs.at[0])
-    for j in range(8):
-        row = xd[j // 4, j % 4 : j % 4 + 1, RED : RED + TAN]
-        level = lax.broadcasted_iota(jnp.int32, (RED, TAN), 0).astype(F32)
-        hot = jnp.where(level == row, 1.0, 0.0)
-        et_buf[:, TAN * j : TAN * (j + 1)] = hot.astype(BF16)
-        e_buf[TAN * j : TAN * (j + 1), :] = jnp.transpose(hot).astype(BF16)
-    x16 = jnp.concatenate([xd[0, 0:4, 0:RED], xd[1, 0:4, 0:RED], jnp.zeros((8, RED), F32)], axis=0)
-    e_buf[ROWS : ROWS + 16, :] = x16.astype(BF16)
-    xt_buf[...] = jnp.transpose(x16).astype(BF16)
-
-    for h in range(2):
+        if h == 0:
+            arrived(xd.at[1 - zl], xrs.at[0])
+            for j in range(8):
+                row = xd[j // 4, j % 4 : j % 4 + 1, RED : RED + TAN]
+                level = lax.broadcasted_iota(jnp.int32, (RED, TAN), 0).astype(F32)
+                hot = jnp.where(level == row, 1.0, 0.0)
+                et_buf[:, TAN * j : TAN * (j + 1)] = hot.astype(BF16)
+                e_buf[TAN * j : TAN * (j + 1), :] = jnp.transpose(hot).astype(BF16)
+            x16 = jnp.concatenate(
+                [xd[0, 0:4, 0:RED], xd[1, 0:4, 0:RED], jnp.zeros((8, RED), F32)], axis=0
+            )
+            e_buf[ROWS : ROWS + 16, :] = x16.astype(BF16)
+            xt_buf[...] = jnp.transpose(x16).astype(BF16)
+            jac[...] = jnp.zeros_like(jac)
+            own_w.wait()
+
+    def relay(h, kind):
         for o in (1, 3, 2):
-            for kind in range(2):
-                piece = wslice(c, kind, lax.rem(mine[kind] + 4 - o, 4), h)
-                arrived(piece, wrs.at[h, kind, o])
-                send(piece, piece, wss.at[h, kind, 4 + o], wrs.at[h, kind, 4 + o], mate)
-    for h in range(2):
-        for o in (0, 1, 3, 2):
-            for kind in range(2):
+            piece = wslice(c, kind, lax.rem(mine[kind] + 4 - o, 4), h)
+            arrived(piece, wrs.at[h, kind, o])
+            send(piece, piece, wss.at[h, kind, 4 + o], wrs.at[h, kind, 4 + o], mate)
+
+    def from_mate(kind):
+        for h in range(2):
+            for o in (0, 1, 3, 2):
                 arrived(wslice(1 - c, kind, lax.rem(mine[kind] + 4 - o, 4), h), wrs.at[h, kind, 4 + o])
-    own_w.wait()
-
-    jac[...] = jnp.zeros_like(jac)
-
-    @pl.loop(0, PART // NC)
-    def _(n):
-        cols = pl.ds(pl.multiple_of(n * NC, NC), NC)
-        p32[...] = nn(e_buf[...], wb[0, :, cols])
-        linear = p32[ROWS : ROWS + 8, :]
+
+    def slopes(linear, cols):
         squash = 1.0 / (1.0 + jnp.exp(-linear))
         slope = squash * (1.0 + linear * (1.0 - squash))
         s1[:, cols] = slope
         s2[:, cols] = squash * (1.0 - squash) * (2.0 + linear * (1.0 - 2.0 * squash))
         hidden = jnp.concatenate([linear * squash, jnp.zeros((8, NC), F32)], axis=0)
         tan[ROWS : ROWS + 16, cols] = hidden.astype(BF16)
+        return slope
+
+    def forward(start):
+        cols = pl.ds(pl.multiple_of(start, NC), NC)
+        p32[...] = nn(e_buf[...], wb[0, :, cols])
+        slope = slopes(p32[ROWS : ROWS + 8, :], cols)
         for j in range(8):
             rows = slice(TAN * j, TAN * (j + 1))
             picked = p32[rows, :]
@@ -227,20 +239,49 @@
             tan[rows, cols] = (slope[j : j + 1, :] * picked).astype(BF16)
         jac[...] += nt(tan[:, cols], wb[1, :, cols])
 
+    relay(0, 0)
+    relay(0, 1)
+    relay(1, 0)
+    forward(HALF * c)
+    relay(1, 1)
+    forward(HALF * c + NC)
+    from_mate(0)
+    forward(HALF * (1 - c))
+    from_mate(1)
+
     own = 2 * zl + zh
     b1 = 2 * (1 - zl) + zh
     b2 = 2 * (1 - zl) + (1 - zh)
     bo = 2 * zl + (1 - zh)
+    lo, hi = pl.ds(0, 128), pl.ds(128, 144)
+    cols = pl.ds(pl.multiple_of(HALF * (1 - c) + NC, NC), NC)
+    tail16 = slice(ROWS, ROWS + 16)
+    slopes(nn(e_buf[tail16, :], wb[0, :, cols])[0:8, :], cols)
+    o16 = jac[tail16, :] + nt(tan[tail16, cols], wb[1, :, cols])
     for b in range(4):
-        o8 = jnp.concatenate([jac[ROWS + 2 * b : ROWS + 2 * b + 2, :], jnp.zeros((14, RED), F32)], axis=0)
-        ox[b] = o8
-        sa[b, 0:256, :] = jac[256 * b : 256 * b + 256, :].astype(BF16)
-        sa[b, 256:272, :] = o8.astype(BF16)
-    lo, hi = pl.ds(0, 128), pl.ds(128, 144)
-    send(sa.at[bo, lo], fa, rss.at[0], rrs.at[0], n1)
-    send(sa.at[bo, hi], fb, rss.at[1], rrs.at[1], n2)
-    send(sa.at[b1, lo], r1.at[lo], rss.at[2], rrs.at[2], n1)
-    send(sa.at[b2, hi], r2.at[hi], rss.at[3], rrs.at[3], n2)
+        o2 = jnp.concatenate([o16[2 * b : 2 * b + 2, :], jnp.zeros((14, RED), F32)], axis=0)
+        ox[b] = o2
+        sa[b, 256:272, :] = o2.astype(BF16)
+    for b, kind in ((bo, 0), (b1, 1), (b2, 2), (own, 3)):
+        rows = pl.ds(pl.multiple_of(256 * b, 256), 256)
+        p32[0:256, :] = nn(e_buf[rows, :], wb[0, :, cols])
+        for e in range(2):
+            half = pl.ds(pl.multiple_of(256 * b + 128 * e, 128), 128)
+            picked = p32[128 * e : 128 * e + 128, :]
+            pk[half, cols] = picked.astype(BF16)
+            tan[half, cols] = (s1[pl.ds(2 * b + e, 1), cols] * picked).astype(BF16)
+        done = jac[rows, :] + nt(tan[rows, cols], wb[1, :, cols])
+        if kind == 3:
+            jac[rows, :] = done
+        else:
+            sa[b, 0:256, :] = done.astype(BF16)
+        if kind == 0:
+            send(sa.at[bo, lo], fa, rss.at[0], rrs.at[0], n1)
+            send(sa.at[bo, hi], fb, rss.at[1], rrs.at[1], n2)
+        elif kind == 1:
+            send(sa.at[b1, lo], r1.at[lo], rss.at[2], rrs.at[2], n1)
+        elif kind == 2:
+            send(sa.at[b2, hi], r2.at[hi], rss.at[3], rrs.at[3], n2)
     arrived(fa, rrs.at[0])
     ca[...] = (sa[b2, 0:128, :].astype(F32) + fa[...].astype(F32)).astype(BF16)
     send(ca, r2.at[lo], rss.at[4], rrs.at[4], n2)
@@ -268,83 +309,126 @@
     mb[own, 256:272, :] = (full - goal).astype(BF16)
     send(mb.at[own, hi], mb.at[own, hi], ass_.at[2], ars.at[2], n1)
     send(mb.at[own, hi], mb.at[own, hi], ass_.at[3], ars.at[3], n2)
+
+    def ends(pair):
+        return [(b, 128 * e, pl.ds(pl.multiple_of(256 * b + 128 * e, 128), 128), 2 * b + e) for b, e in pair]
+
+    def turn(pair):
+        for k, (b, at, _, _) in enumerate(ends(pair)):
+            mt[:, 128 * k : 128 * k + 128] = jnp.transpose(mb[b, at : at + 128, :])
+            lm[128 * k : 128 * k + 128, :] = mb[b, at : at + 128, :]
+
+    def picked_grads(pair, cot, cols):
+        parts = []
+        for k, (_, _, rows, j) in enumerate(ends(pair)):
+            ct = cot[128 * k : 128 * k + 128, :].astype(BF16).astype(F32)
+            pr[pl.ds(j, 1), cols] = jnp.sum(ct * pk[rows, cols].astype(F32), axis=0, keepdims=True)
+            parts.append((ct * s1[pl.ds(j, 1), cols]).astype(BF16))
+        return jnp.concatenate(parts, axis=0)
+
+    def tangents(pair, cols):
+        return jnp.concatenate([tan[rows, cols] for _, _, rows, _ in ends(pair)], axis=0)
+
+    def hot_columns(pair):
+        return jnp.concatenate([et_buf[:, rows] for _, _, rows, _ in ends(pair)], axis=1)
+
+    def backward(pair, first):
+        turn(pair)
+
+        @pl.loop(0, PART // NC)
+        def _(n):
+            cols = pl.ds(pl.multiple_of(n * NC, NC), NC)
+            last = nn(mt[...], tangents(pair, cols))
+            g[1, :, cols] = last if first else g[1, :, cols] + last
+            p32[0:256, :] = nn(lm[0:256, :], wb[1, :, cols])
+            new = nn(hot_columns(pair), picked_grads(pair, p32[0:256, :], cols))
+            g[0, :, cols] = new if first else g[0, :, cols] + new
+
+    backward(((own, 0), (own, 1)), True)
     arrived(mb.at[b1, lo], ars.at[0])
     send(mb.at[b1, lo], mb.at[b1, lo], ass_.at[4], ars.at[4], n2)
+    arrived(mb.at[b2, lo], ars.at[1])
+    backward(((b1, 0), (b2, 0)), False)
     arrived(mb.at[b2, hi], ars.at[3])
     send(mb.at[b2, hi], mb.at[b2, hi], ass_.at[5], ars.at[5], n1)
-    arrived(mb.at[b2, lo], ars.at[1])
     arrived(mb.at[b1, hi], ars.at[2])
+    backward(((b1, 1), (b2, 1)), False)
     arrived(mb.at[bo, lo], ars.at[4])
     arrived(mb.at[bo, hi], ars.at[5])
 
-    for b in range(4):
-        mt[:, 256 * b : 256 * b + 256] = jnp.transpose(mb[b, 0:256, :])
+    tail = ((bo, 0), (bo, 1))
+    turn(tail)
     heads = [mb[b, 256:272, :].astype(F32)[0:2, :] for b in range(4)]
     m16 = jnp.concatenate(heads + [jnp.zeros((8, RED), F32)], axis=0)
-    mx[...] = m16.astype(BF16)
+    lm[256:272, :] = m16.astype(BF16)
     mxt[...] = jnp.transpose(m16).astype(BF16)
-
-    def grads(start):
-        cols = pl.ds(pl.multiple_of(start, NC), NC)
-        last = nn(mt[...], tan[0:ROWS, cols]) + nn(mxt[...], tan[ROWS : ROWS + 16, cols])
-        g32[1] = last
-        w1 = wb[1, :, cols]
-        for b in range(4):
-            p32[256 * b : 256 * b + 256, :] = nn(mb[b, 0:256, :], w1)
-        cx = nn(mx[...], w1).astype(BF16).astype(F32)
-        pre = []
-        for j in range(8):
-            rows = slice(TAN * j, TAN * (j + 1))
-            ct = p32[rows, :].astype(BF16).astype(F32)
-            slope = s1[j : j + 1, cols]
-            projected = jnp.sum(ct * pk[rows, cols].astype(F32), axis=0, keepdims=True)
-            pre.append(cx[j : j + 1, :] * slope + s2[j : j + 1, cols] * projected)
-            rbuf[rows, :] = (ct * slope).astype(BF16)
-        pre16 = jnp.concatenate(pre + [jnp.zeros((8, NC), F32)], axis=0).astype(BF16)
-        g32[0] = nn(et_buf[...], rbuf[...]) + nn(xt_buf[...], pre16)
-
-    lr = 32
-    for q in range(4):
-        if q < 2:
-            grads(HALF * (1 - c) + NC * q)
-            ds[q] = g32[...].astype(BF16)
-            send(ds.at[q], dr.at[q], dss.at[q], drs.at[q], mate)
-            continue
-        q = q - 2
-        grads(HALF * c + NC * q)
-        arrived(dr.at[q], drs.at[q])
-        total = g32[...] + dr[q].astype(F32)
-        a32[q] = total.reshape(2, 4, 4, lr, NC)
-        gst[q] = total.astype(BF16).reshape(2, 4, 4, lr, NC)
-        for o in (2, 1, 3):
-            if q == 0:
-                src, to = gst.at[q, :, xpeer(o)], dev(px=xpeer(o))
-            else:
-                src, to = gst.at[q, :, :, ypeer(o)], dev(py=ypeer(o))
-            send(src, p1r.at[q, o - 1], p1s.at[q, o - 1], p1q.at[q, o - 1], to)
+    for half in range(2):
+        for q in range(2):
+            base = HALF * (1 - c) if half == 0 else HALF * c
+            cols = pl.ds(pl.multiple_of(base + NC * q, NC), NC)
+            for layer in (1, 0):
+                if layer == 1:
+                    total = nn(mt[...], tangents(tail, cols)) + nn(mxt[...], tan[tail16, cols])
+                else:
+                    p32[0:272, :] = nn(lm[...], wb[1, :, cols])
+                    r = picked_grads(tail, p32[0:256, :], cols)
+                    cx = p32[256:264, :].astype(BF16).astype(F32)
+                    pre = cx * s1[:, cols] + s2[:, cols] * pr[:, cols]
+                    pre = jnp.concatenate([pre, jnp.zeros((8, NC), F32)], axis=0).astype(BF16)
+                    total = nn(hot_columns(tail), r) + nn(xt_buf[...], pre)
+                if half == 0:
+                    ds[q, layer] = (g[layer, :, cols] + total).astype(BF16)
+                    send(ds.at[q, layer], dr.at[q, layer], dss.at[q, layer], drs.at[q, layer], mate)
+                    continue
+                g[layer, :, cols] += total
+                arrived(dr.at[q, layer], drs.at[q, layer])
+                total = g[layer, :, cols] + dr[q, layer].astype(F32)
+                g[layer, :, cols] = total
+                gst[q, layer] = total.astype(BF16).reshape(4, 4, 32, NC)
+                for o in (2, 1, 3):
+                    if layer == 1:
+                        src, to = gst.at[q, layer, xpeer(o)], dev(px=xpeer(o))
+                    else:
+                        src, to = gst.at[q, layer, :, ypeer(o)], dev(py=ypeer(o))
+                    send(
+                        src,
+                        p1r.at[q, layer, o - 1],
+                        p1s.at[q, layer, o - 1],
+                        p1q.at[q, layer, o - 1],
+                        to,
+                    )
 
     for q in range(2):
-        for o in (1, 3, 2):
-            arrived(p1r.at[q, o - 1], p1q.at[q, o - 1])
-        total = a32[q, :, x] if q == 0 else a32[q, :, :, y]
-        for o in (1, 3, 2):
-            total = total + p1r[q, o - 1].astype(F32)
-        hst[q] = total.astype(BF16)
-        g32[0, 256 * q : 256 * q + 256, :] = total.reshape(256, NC)
-        for o in (2, 1, 3):
-            if q == 0:
-                src, to = hst.at[q, :, ypeer(o)], dev(py=ypeer(o))
-            else:
-                src, to = hst.at[q, :, xpeer(o)], dev(px=xpeer(o))
-            send(src, p2r.at[q, o - 1], p2s.at[q, o - 1], p2q.at[q, o - 1], to)
+        cols = pl.ds(pl.multiple_of(HALF * c + NC * q, NC), NC)
+        for layer in (1, 0):
+            for o in (1, 3, 2):
+                arrived(p1r.at[q, layer, o - 1], p1q.at[q, layer, o - 1])
+            for k in range(4):
+                rows = 128 * x + 32 * k if layer == 1 else 128 * k + 32 * y
+                total = g[layer, pl.ds(pl.multiple_of(rows, 32), 32), cols]
+                for o in (1, 3, 2):
+                    total = total + p1r[q, layer, o - 1, k].astype(F32)
+                hst[q, layer, k] = total.astype(BF16)
+                h32[q, layer, k] = total
+            for o in (2, 1, 3):
+                if layer == 1:
+                    src, to = hst.at[q, layer, ypeer(o)], dev(py=ypeer(o))
+                else:
+                    src, to = hst.at[q, layer, xpeer(o)], dev(px=xpeer(o))
+                send(
+                    src,
+                    p2r.at[q, layer, o - 1],
+                    p2s.at[q, layer, o - 1],
+                    p2q.at[q, layer, o - 1],
+                    to,
+                )
     for q in range(2):
-        for o in (1, 3, 2):
-            arrived(p2r.at[q, o - 1], p2q.at[q, o - 1])
-        keep = y if q == 0 else x
-        for layer in range(2):
-            total = g32[0, pl.ds(pl.multiple_of(256 * q + 128 * layer + lr * keep, lr), lr), :]
+        for layer in (1, 0):
             for o in (1, 3, 2):
-                total = total + p2r[q, o - 1, layer].astype(F32)
+                arrived(p2r.at[q, layer, o - 1], p2q.at[q, layer, o - 1])
+            total = h32[q, layer, y if layer == 1 else x]
+            for o in (1, 3, 2):
+                total = total + p2r[q, layer, o - 1].astype(F32)
             fs[layer, :, NC * q : NC * (q + 1)] = total
 
     where = pl.ds(pl.multiple_of(PART * z + HALF * c, HALF), HALF)
@@ -386,9 +470,12 @@
     result = pl.pallas_call(
         kernel,
         out_shape=jax.ShapeDtypeStruct((8, WIDTH), F32),
-        in_specs=[pl.BlockSpec(memory_space=pltpu.SMEM), vmem, vmem, vmem, anywhere, anywhere],
+        in_specs=[pl.BlockSpec(memory_space=pltpu.SMEM)] + [anywhere] * 5,
         out_specs=vmem,
         scratch_shapes=[
+            v((POOL, RED), BF16),
+            v((POOL, TAN), jnp.int32),
+            v((POOL, RED), BF16),
             v((2, RED, PART), BF16),
             v((POOL, TAN, RED), BF16),
             v((POOL, RED), F32),
@@ -413,20 +500,20 @@
             v((272, RED), BF16),
             v((272, RED), BF16),
             v((4, 272, RED), BF16),
-            v((RED, ROWS), BF16),
+            v((RED, 256), BF16),
             v((RED, 16), BF16),
-            v((16, RED), BF16),
-            v((ROWS, NC), BF16),
+            v((272, RED), BF16),
+            v((8, PART), F32),
+            v((2, RED, PART), F32),
             v((2, 2, RED, NC), BF16),
             v((2, 2, RED, NC), BF16),
-            v((2, RED, NC), F32),
             v((2, 2, 4, 4, 32, NC), BF16),
-            v((2, 3, 2, 4, 32, NC), BF16),
-            v((2, 2, 4, 4, 32, NC), F32),
+            v((2, 2, 3, 4, 32, NC), BF16),
             v((2, 2, 4, 32, NC), BF16),
-            v((2, 3, 2, 32, NC), BF16),
+            v((2, 2, 4, 32, NC), F32),
+            v((2, 2, 3, 32, NC), BF16),
             v((2, 32, HALF), F32),
-            dma((2,)),
+            dma((5,)),
             dma((2, 2, 8)),
             dma((2, 2, 8)),
             dma((1,)),
@@ -435,12 +522,12 @@
             dma((6,)),
             dma((6,)),
             dma((6,)),
-            dma((2,)),
-            dma((2,)),
-            dma((2, 3)),
-            dma((2, 3)),
-            dma((2, 3)),
-            dma((2, 3)),
+            dma((2, 2)),
+            dma((2, 2)),
+            dma((2, 2, 3)),
+            dma((2, 2, 3)),
+            dma((2, 2, 3)),
+            dma((2, 2, 3)),
             dma((7,)),
             dma((7,)),
         ],

time: 89.9 us -> 79.6 us (0.89)
  Pallas kernels: 88 us -> 77.8 us
    pallas_call x1, Pallas kernels: 88 us -> 77.8 us  [shards(): pl.pallas_call(kernel, out_shape=jax.ShapeDtypeStruct((8, WIDTH), F32), i...]
where the time goes in v2:
time: 79.6 us; the launch traced here: 79.5 us
  Pallas kernels  77.8 us (98%)
  local copies, waits for them, and re-layouts  1.67 us (2%)
    pallas_call x1, Pallas kernels, shards(): pl.pallas_call(kernel, out_shape=jax.ShapeDtypeStruct((8, WIDTH), F32), i...  77.8 us
    unnamed x1, local copies, waits for them, and re-layouts  1.67 us

profile of v2, /device:TPU:1, one launch (start us, length us, event | category | flops | bytes accessed | tf_op | source)
XLA Modules:
  0.0 79.5 jit_solution(18197481232888161902)
XLA Ops:
  0.0 77.8 %step.1 = f32[8,8192]{1,0:T(8,128)} custom-call(s32[1,8]{1,0:T(1,128)} %plan.1, bf16[8,512]{1,0:T(8,128)(2,1)} %samples_hbm.1, s32[8,128]{1,0:T(8,128)} %dirs_hbm.1, bf16[8,512]{1,0:T(8,128)(2,1)} %targets_hbm.1, bf16[8,128,512]{2,1,0:T(8,128)(2,1)} %jt_hbm.1, bf16[1,512,8192]{2,1,0:T(8,128)(2,1)} %w_hbm.1), custom_call_target="tpu_custom_call" | custom-call | tf_op jit(solution)/shard_map/step/pallas_call | solution.py:470
  77.8 1.7 %copy.8 = f32[1,8,8192]{2,1,0:T(8,128)} copy(f32[1,8,8192]{2,1,0:T(8,128)} %bitcast.1) | data formatting | bytes 524288

commit v3 on v2

v3 whole, which is shorter than its diff:
```python
import jax
import jax.numpy as jnp
from jax import lax
from jax.experimental import pallas as pl
from jax.experimental.pallas import tpu as pltpu
from jax.sharding import Mesh
from jax.sharding import PartitionSpec as P

AXES = ("x", "y", "zl", "c", "zh")
DP = ("x", "y", "zl", "c")
F32 = jnp.float32
BF16 = jnp.bfloat16
MESH = pl.DeviceIdType.MESH

RED = 512
WIDTH = 8192
TAN = 128
MICRO = 4
POOL = 8
PART = WIDTH // 4
HALF = PART // 2
ROWS = 8 * TAN
NC = 512
JAC = 32.0
LIMIT = 60 * 1024 * 1024


def nn(a, b):
    return lax.dot_general(a, b, (((1,), (0,)), ((), ())), preferred_element_type=F32)


def nt(a, b):
    return lax.dot_general(a, b, (((1,), (1,)), ((), ())), preferred_element_type=F32)


def kernel(
    plan_hbm,
    samples_hbm,
    dirs_hbm,
    targets_hbm,
    jt_hbm,
    w_hbm,
    out,
    plan,
    samples,
    dirs,
    targets,
    wst,
    wb,
    jt,
    s32,
    d32,
    t32,
    xd,
    e_buf,
    et_buf,
    xt_buf,
    p32,
    pk,
    tan,
    s1,
    s2,
    jac,
    ox,
    sa,
    fa,
    fb,
    ca,
    cb,
    r1,
    r2,
    mb,
    mt,
    mxt,
    lm,
    pr,
    g,
    ds,
    dr,
    gst,
    f1,
    cmb,
    p1r,
    hst,
    h32,
    p2r,
    fs,
    like,
    lsem,
    wss,
    wrs,
    xss,
    xrs,
    rss,
    rrs,
    ass_,
    ars,
    dss,
    drs,
    p1s,
    p1q,
    p2s,
    p2q,
    p3s,
    p3q,
):
    x = lax.axis_index("x")
    y = lax.axis_index("y")
    zl = lax.axis_index("zl")
    c = lax.axis_index("c")
    zh = lax.axis_index("zh")
    z = 2 * zh + zl

    def dev(px=x, py=y, pzl=zl, pc=c, pzh=zh):
        return (px, py, pzl, pc, pzh)

    def xpeer(o):
        return lax.rem(x + o, 4)

    def ypeer(o):
        return lax.rem(y + o, 4)

    n1 = dev(pzl=1 - zl)
    n2 = dev(pzl=1 - zl, pzh=1 - zh)
    mate = dev(pc=1 - c)
    here = dev()

    def send(src, dst, ssem, rsem, where):
        copy = pltpu.make_async_remote_copy(
            src_ref=src, dst_ref=dst, send_sem=ssem, recv_sem=rsem, device_id=where, device_id_type=MESH
        )
        copy.start()

    def arrived(dst, rsem):
        pltpu.make_async_remote_copy(
            src_ref=dst, dst_ref=dst, send_sem=rsem, recv_sem=rsem, device_id=here, device_id_type=MESH
        ).wait_recv()

    def sent(like, ssem):
        pltpu.make_async_remote_copy(
            src_ref=like, dst_ref=like, send_sem=ssem, recv_sem=ssem, device_id=here, device_id_type=MESH
        ).wait_send()

    barrier = pltpu.get_barrier_semaphore()
    peers = [n1, n2, dev(pzh=1 - zh)]
    peers += [dev(pzl=a, pc=1 - c, pzh=b) for a in range(2) for b in range(2)]
    peers += [dev(px=xpeer(o)) for o in (1, 2, 3)]
    peers += [dev(py=ypeer(o)) for o in (1, 2, 3)]
    for peer in peers:
        pl.semaphore_signal(barrier, inc=1, device_id=peer, device_id_type=MESH)

    small = []
    pieces = ((plan_hbm, plan), (samples_hbm, samples), (dirs_hbm, dirs), (targets_hbm, targets))
    for k, (src, dst) in enumerate(pieces):
        small.append(pltpu.make_async_copy(src, dst, lsem.at[2 + k]))
        small[-1].start()
    mine = (x, y)
    for k in range(4):
        for kind in range(2):
            first = pl.multiple_of(PART * (3 - z) + 512 * k + 256 * c + 128 * kind, 128)
            src = w_hbm.at[0, pl.ds(pl.multiple_of(128 * mine[kind], 128), 128), pl.ds(first, 128)]
            pltpu.make_async_copy(src, wst.at[k, kind], lsem.at[6]).start()
    own_w = pltpu.make_async_copy(
        w_hbm.at[0, :, pl.ds(pl.multiple_of(PART * z, PART), PART)], wb.at[zh], lsem.at[0]
    )
    own_w.start()
    own_j = pltpu.make_async_copy(jt_hbm, jt, lsem.at[1])
    own_j.start()

    for copy in small:
        copy.wait()
    s32[...] = samples[...].astype(F32)
    d32[...] = dirs[...].astype(F32)
    t32[...] = targets[...].astype(F32)
    xd[zl, MICRO:8, :] = jnp.zeros((8 - MICRO, RED + TAN), F32)
    for i in range(MICRO):
        at = plan[0, i]
        xd[zl, i : i + 1, 0:RED] = s32[pl.ds(at, 1), :]
        xd[zl, i : i + 1, RED : RED + TAN] = d32[pl.ds(at, 1), :]

    pltpu.make_async_copy(wst, wst, lsem.at[6]).wait()
    pl.semaphore_wait(barrier, len(peers))

    def wslice(layer, core, k, kind, place):
        rows = pl.ds(pl.multiple_of(128 * place, 128), 128)
        return wb.at[layer, rows, pl.ds(pl.multiple_of(512 * k + 256 * core + 128 * kind, 128), 128)]

    for k in range(4):
        for kind in range(2):
            send(
                wst.at[k, kind],
                wslice(zh, c, k, kind, mine[kind]),
                wss.at[0],
                wrs.at[2 * k + kind],
                n2,
            )
        if k == 0:
            send(xd.at[zl], xd.at[zl], xss.at[0], xrs.at[0], n1)

    def from_z(k):
        for kind in range(2):
            piece = wslice(1 - zh, c, k, kind, mine[kind])
            arrived(piece, wrs.at[2 * k + kind])
            for o in (1, 3, 2):
                to = dev(px=xpeer(o)) if kind == 0 else dev(py=ypeer(o))
                send(piece, piece, wss.at[0], wrs.at[8 + 2 * k + (o == 2)], to)
            send(piece, piece, wss.at[0], wrs.at[16 + k], mate)

    def relay(k):
        for group in ((1, 3), (2,)):
            arrived(wb.at[1 - zh, pl.ds(0, 128), pl.ds(0, 256 * len(group))], wrs.at[8 + 2 * k + len(group) % 2])
            for o in group:
                for kind in range(2):
                    piece = wslice(1 - zh, c, k, kind, lax.rem(mine[kind] + 4 - o, 4))
                    send(piece, piece, wss.at[0], wrs.at[16 + k], mate)

    def from_mate(k):
        arrived(wb.at[1 - zh, :, pl.ds(pl.multiple_of(512 * k + 256 * (1 - c), 256), 256)], wrs.at[16 + k])

    from_z(0)
    from_z(1)
    arrived(xd.at[1 - zl], xrs.at[0])
    for j in range(8):
        row = xd[j // 4, j % 4 : j % 4 + 1, RED : RED + TAN]
        level = lax.broadcasted_iota(jnp.int32, (RED, TAN), 0).astype(F32)
        hot = jnp.where(level == row, 1.0, 0.0)
        et_buf[:, TAN * j : TAN * (j + 1)] = hot.astype(BF16)
        e_buf[TAN * j : TAN * (j + 1), :] = jnp.transpose(hot).astype(BF16)
    x16 = jnp.concatenate([xd[0, 0:4, 0:RED], xd[1, 0:4, 0:RED], jnp.zeros((8, RED), F32)], axis=0)
    e_buf[ROWS : ROWS + 16, :] = x16.astype(BF16)
    xt_buf[...] = jnp.transpose(x16).astype(BF16)
    jac[...] = jnp.zeros_like(jac)
    own_w.wait()

    def slopes(linear, cols):
        squash = 1.0 / (1.0 + jnp.exp(-linear))
        slope = squash * (1.0 + linear * (1.0 - squash))
        s1[:, cols] = slope
        s2[:, cols] = squash * (1.0 - squash) * (2.0 + linear * (1.0 - 2.0 * squash))
        hidden = jnp.concatenate([linear * squash, jnp.zeros((8, NC), F32)], axis=0)
        tan[ROWS : ROWS + 16, cols] = hidden.astype(BF16)
        return slope

    def forward(start):
        cols = pl.ds(pl.multiple_of(start, NC), NC)
        p32[...] = nn(e_buf[...], wb[0, :, cols])
        slope = slopes(p32[ROWS : ROWS + 8, :], cols)
        for j in range(8):
            rows = slice(TAN * j, TAN * (j + 1))
            picked = p32[rows, :]
            pk[rows, cols] = picked.astype(BF16)
            tan[rows, cols] = (slope[j : j + 1, :] * picked).astype(BF16)
        jac[...] += nt(tan[:, cols], wb[1, :, cols])

    from_z(2)
    relay(0)
    from_z(3)
    relay(1)
    from_mate(0)
    forward(0)
    relay(2)
    from_mate(1)
    forward(NC)
    relay(3)
    from_mate(2)
    forward(2 * NC)
    from_mate(3)

    own = 2 * zl + zh
    b1 = 2 * (1 - zl) + zh
    b2 = 2 * (1 - zl) + (1 - zh)
    bo = 2 * zl + (1 - zh)
    lo, hi = pl.ds(0, 128), pl.ds(128, 144)
    cols = pl.ds(3 * NC, NC)
    tail16 = slice(ROWS, ROWS + 16)
    slopes(nn(e_buf[tail16, :], wb[0, :, cols])[0:8, :], cols)
    o16 = jac[tail16, :] + nt(tan[tail16, cols], wb[1, :, cols])
    for b in range(4):
        o2 = jnp.concatenate([o16[2 * b : 2 * b + 2, :], jnp.zeros((14, RED), F32)], axis=0)
        ox[b] = o2
        sa[b, 256:272, :] = o2.astype(BF16)
    for b, kind in ((bo, 0), (b1, 1), (b2, 2), (own, 3)):
        rows = pl.ds(pl.multiple_of(256 * b, 256), 256)
        p32[0:256, :] = nn(e_buf[rows, :], wb[0, :, cols])
        for e in range(2):
            half = pl.ds(pl.multiple_of(256 * b + 128 * e, 128), 128)
            picked = p32[128 * e : 128 * e + 128, :]
            pk[half, cols] = picked.astype(BF16)
            tan[half, cols] = (s1[pl.ds(2 * b + e, 1), cols] * picked).astype(BF16)
        done = jac[rows, :] + nt(tan[rows, cols], wb[1, :, cols])
        if kind == 3:
            jac[rows, :] = done
        else:
            sa[b, 0:256, :] = done.astype(BF16)
        if kind == 0:
            send(sa.at[bo, lo], fa, rss.at[0], rrs.at[0], n1)
            send(sa.at[bo, hi], fb, rss.at[0], rrs.at[1], n2)
        elif kind == 1:
            send(sa.at[b1, lo], r1.at[lo], rss.at[0], rrs.at[2], n1)
        elif kind == 2:
            send(sa.at[b2, hi], r2.at[hi], rss.at[0], rrs.at[3], n2)
    arrived(fa, rrs.at[0])
    ca[...] = (sa[b2, 0:128, :].astype(F32) + fa[...].astype(F32)).astype(BF16)
    send(ca, r2.at[lo], rss.at[0], rrs.at[4], n2)
    arrived(fb, rrs.at[1])
    cb[...] = (sa[b1, 128:272, :].astype(F32) + fb[...].astype(F32)).astype(BF16)
    send(cb, r1.at[hi], rss.at[0], rrs.at[5], n1)

    own_j.wait()
    arrived(r1.at[lo], rrs.at[2])
    arrived(r2.at[lo], rrs.at[4])
    p0 = plan[0, 2 * zh]
    p1 = plan[0, 2 * zh + 1]
    full = jac[pl.ds(pl.multiple_of(256 * own, 256), 128), :]
    full = full + r1[0:128, :].astype(F32) + r2[0:128, :].astype(F32)
    mb[own, 0:128, :] = (JAC * (full - jt[p0].astype(F32))).astype(BF16)
    send(mb.at[own, lo], mb.at[own, lo], ass_.at[0], ars.at[0], n1)
    arrived(r2.at[hi], rrs.at[3])
    arrived(r1.at[hi], rrs.at[5])
    full = jac[pl.ds(pl.multiple_of(256 * own + 128, 128), 128), :]
    full = full + r1[128:256, :].astype(F32) + r2[128:256, :].astype(F32)
    mb[own, 128:256, :] = (JAC * (full - jt[p1].astype(F32))).astype(BF16)
    full = ox[own] + r1[256:272, :].astype(F32) + r2[256:272, :].astype(F32)
    goal = jnp.concatenate([t32[pl.ds(p0, 1), :], t32[pl.ds(p1, 1), :], jnp.zeros((14, RED), F32)], axis=0)
    mb[own, 256:272, :] = (full - goal).astype(BF16)
    send(mb.at[own, hi], mb.at[own, hi], ass_.at[0], ars.at[3], n2)
    send(mb.at[own, lo], mb.at[own, lo], ass_.at[0], ars.at[1], n2)
    send(mb.at[own, hi], mb.at[own, hi], ass_.at[0], ars.at[2], n1)

    def ends(pair):
        return [(b, 128 * e, pl.ds(pl.multiple_of(256 * b + 128 * e, 128), 128), 2 * b + e) for b, e in pair]

    def turn(pair):
        for k, (b, at, _, _) in enumerate(ends(pair)):
            mt[:, 128 * k : 128 * k + 128] = jnp.transpose(mb[b, at : at + 128, :])
            lm[128 * k : 128 * k + 128, :] = mb[b, at : at + 128, :]

    def picked_grads(pair, cot, cols):
        parts = []
        for k, (_, _, rows, j) in enumerate(ends(pair)):
            ct = cot[128 * k : 128 * k + 128, :].astype(BF16).astype(F32)
            pr[pl.ds(j, 1), cols] = jnp.sum(ct * pk[rows, cols].astype(F32), axis=0, keepdims=True)
            parts.append((ct * s1[pl.ds(j, 1), cols]).astype(BF16))
        return jnp.concatenate(parts, axis=0)

    def tangents(pair, cols):
        return jnp.concatenate([tan[rows, cols] for _, _, rows, _ in ends(pair)], axis=0)

    def hot_columns(pair):
        return jnp.concatenate([et_buf[:, rows] for _, _, rows, _ in ends(pair)], axis=1)

    def add_to(layer, cols, new, first=False):
        g[layer, :, cols] = new if first else g[layer, :, cols] + new

    def backward(pair, first):
        turn(pair)
        chunks = [pl.ds(NC * n, NC) for n in range(PART // NC)]

        def cotangents(n):
            p32[512 * (n % 2) : 512 * (n % 2) + 256, :] = nn(lm[0:256, :], wb[1, :, chunks[n]])

        cotangents(0)
        for n, cols in enumerate(chunks):
            if n + 1 < len(chunks):
                cotangents(n + 1)
            add_to(1, cols, nn(mt[...], tangents(pair, cols)), first)
            r = picked_grads(pair, p32[512 * (n % 2) : 512 * (n % 2) + 256, :], cols)
            add_to(0, cols, nn(hot_columns(pair), r), first)

    backward(((own, 0), (own, 1)), True)
    arrived(mb.at[b1, lo], ars.at[0])
    send(mb.at[b1, lo], mb.at[b1, lo], ass_.at[0], ars.at[4], n2)
    arrived(mb.at[b2, hi], ars.at[3])
    send(mb.at[b2, hi], mb.at[b2, hi], ass_.at[0], ars.at[5], n1)
    backward(((b1, 0), (b2, 1)), False)
    arrived(mb.at[b2, lo], ars.at[1])
    arrived(mb.at[b1, hi], ars.at[2])
    backward(((b1, 1), (b2, 0)), False)
    arrived(mb.at[bo, lo], ars.at[4])
    arrived(mb.at[bo, hi], ars.at[5])

    tail = ((bo, 0), (bo, 1))
    turn(tail)
    heads = [mb[b, 256:272, :].astype(F32)[0:2, :] for b in range(4)]
    m16 = jnp.concatenate(heads + [jnp.zeros((8, RED), F32)], axis=0)
    lm[256:272, :] = m16.astype(BF16)
    mxt[...] = jnp.transpose(m16).astype(BF16)

    def ahead(layer):
        return xpeer(1) if layer == 1 else ypeer(1)

    def behind(layer):
        return xpeer(3) if layer == 1 else ypeer(3)

    def at_place(layer, place):
        return dev(px=place) if layer == 1 else dev(py=place)

    def half_for(q, layer, place, part):
        if layer == 1:
            return gst.at[q, layer, place, pl.ds(2 * part, 2)]
        return gst.at[q, layer, pl.ds(2 * part, 2), place]

    def rows_for(layer, place, k):
        at = 128 * place + 32 * k if layer == 1 else 128 * k + 32 * place
        return pl.ds(pl.multiple_of(at, 32), 32)

    def start_unit(q, layer):
        across = xpeer(2) if layer == 1 else ypeer(2)
        up, down = ahead(layer), behind(layer)
        moves = (
            (half_for(q, layer, across, 0), f1.at[q, layer, 0], up),
            (half_for(q, layer, across, 1), f1.at[q, layer, 1], down),
            (half_for(q, layer, up, 1), p1r.at[q, layer, 0, pl.ds(2, 2)], up),
            (half_for(q, layer, down, 0), p1r.at[q, layer, 1, pl.ds(0, 2)], down),
        )
        for k, (src, dst, place) in enumerate(moves):
            send(src, dst, p1s.at[0], p1q.at[q, layer, min(k, 2)], at_place(layer, place))

    def forward_unit(q, layer):
        cols = pl.ds(pl.multiple_of(HALF * c + NC * q, NC), NC)
        for part, place in ((0, ahead(layer)), (1, behind(layer))):
            arrived(f1.at[q, layer, part], p1q.at[q, layer, part])
            for k in range(2):
                total = g[layer, rows_for(layer, place, 2 * part + k), cols]
                cmb[q, layer, part, k] = (total + f1[q, layer, part, k].astype(F32)).astype(BF16)
            send(
                cmb.at[q, layer, part],
                p1r.at[q, layer, part, pl.ds(2 * part, 2)],
                p1s.at[0],
                p1q.at[q, layer, 2],
                at_place(layer, place),
            )

    units = []
    for half in range(2):
        for q in range(2):
            base = HALF * (1 - c) if half == 0 else HALF * c
            units.append((half, q, pl.ds(pl.multiple_of(base + NC * q, NC), NC)))

    def leave(half, q, layer, cols, total):
        if half == 0:
            ds[q, layer] = (g[layer, :, cols] + total).astype(BF16)
            send(ds.at[q, layer], dr.at[q, layer], dss.at[0], drs.at[q, layer], mate)
        else:
            g[layer, :, cols] += total

    def tail_cotangents(n):
        p32[512 * (n % 2) : 512 * (n % 2) + 272, :] = nn(lm[...], wb[1, :, units[n][2]])

    tail_cotangents(0)
    for n, (half, q, cols) in enumerate(units):
        if n + 1 < len(units):
            tail_cotangents(n + 1)
        total = nn(mt[...], tangents(tail, cols)) + nn(mxt[...], tan[tail16, cols])
        leave(half, q, 1, cols, total)
        at = 512 * (n % 2)
        r = picked_grads(tail, p32[at : at + 256, :], cols)
        cx = p32[at + 256 : at + 264, :].astype(BF16).astype(F32)
        pre = cx * s1[:, cols] + s2[:, cols] * pr[:, cols]
        pre = jnp.concatenate([pre, jnp.zeros((8, NC), F32)], axis=0).astype(BF16)
        leave(half, q, 0, cols, nn(hot_columns(tail), r) + nn(xt_buf[...], pre))
        if half == 0:
            continue
        for layer in (1, 0):
            arrived(dr.at[q, layer], drs.at[q, layer])
            total = g[layer, :, cols] + dr[q, layer].astype(F32)
            g[layer, :, cols] = total
            gst[q, layer] = total.astype(BF16).reshape(4, 4, 32, NC)
            start_unit(q, layer)

    for q in range(2):
        for layer in (1, 0):
            forward_unit(q, layer)
    for q in range(2):
        cols = pl.ds(pl.multiple_of(HALF * c + NC * q, NC), NC)
        for layer in (1, 0):
            arrived(p1r.at[q, layer], p1q.at[q, layer, 2])
            for k in range(4):
                total = g[layer, rows_for(layer, x if layer == 1 else y, k), cols]
                for side in range(2):
                    total = total + p1r[q, layer, side, k].astype(F32)
                hst[q, layer, k] = total.astype(BF16)
                h32[q, layer, k] = total
            for o in (2, 1, 3):
                if layer == 1:
                    src, to = hst.at[q, layer, ypeer(o)], dev(py=ypeer(o))
                else:
                    src, to = hst.at[q, layer, xpeer(o)], dev(px=xpeer(o))
                send(
                    src,
                    p2r.at[q, layer, o - 1],
                    p2s.at[0],
                    p2q.at[q, layer],
                    to,
                )

    others = [(a, b, d) for a in (1, 0) for b in (1, 0) for d in (1, 0) if a + b + d]

    def moved(step):
        pzh, pzl, pc = (lax.rem(a + b, 2) for a, b in zip((zh, zl, c), step))
        return pzh, pzl, pc

    def out_at(pzh, pzl, pc, q):
        return pl.ds(pl.multiple_of(PART * (2 * pzh + pzl) + HALF * pc + NC * q, NC), NC)

    for q in range(2):
        for layer in (1, 0):
            arrived(p2r.at[q, layer], p2q.at[q, layer])
            total = h32[q, layer, y if layer == 1 else x]
            for o in (1, 3, 2):
                total = total + p2r[q, layer, o - 1].astype(F32)
            for k in range(4):
                fs[q, layer, k] = total[8 * k : 8 * k + 8, :].astype(BF16)
        for step in others:
            pzh, pzl, pc = moved(step)
            send(
                fs.at[q, pzh, 2 * pzl + pc],
                out.at[:, out_at(zh, zl, c, q)],
                p3s.at[0],
                p3q.at[0],
                dev(pzl=pzl, pc=pc, pzh=pzh),
            )
        pltpu.make_async_copy(fs.at[q, zh, 2 * zl + c], out.at[:, out_at(zh, zl, c, q)], lsem.at[7]).start()
    arrived(like, p3q.at[0])
    pltpu.make_async_copy(fs.at[0, 0, pl.ds(0, 2)], fs.at[0, 0, pl.ds(0, 2)], lsem.at[7]).wait()
    sent(wb.at[0], wss.at[0])
    sent(xd.at[0], xss.at[0])
    sent(sa.at[pl.ds(0, 3)], rss.at[0])
    sent(mb.at[pl.ds(0, 3)], ass_.at[0])
    sent(ds, dss.at[0])
    sent(gst.at[:, :, pl.ds(0, 3)], p1s.at[0])
    sent(p2r, p2s.at[0])
    sent(like, p3s.at[0])


def shards(samples, targets, jacobian_targets, directions, plan, weights):
    anywhere = pl.BlockSpec(memory_space=pl.ANY)
    dma = pltpu.SemaphoreType.DMA
    v = pltpu.VMEM
    result = pl.pallas_call(
        kernel,
        out_shape=jax.ShapeDtypeStruct((8, WIDTH), BF16),
        in_specs=[anywhere] * 6,
        out_specs=anywhere,
        scratch_shapes=[
            pltpu.SMEM((1, POOL), jnp.int32),
            v((POOL, RED), BF16),
            v((POOL, TAN), jnp.int32),
            v((POOL, RED), BF16),
            v((4, 2, 128, 128), BF16),
            v((2, RED, PART), BF16),
            v((POOL, TAN, RED), BF16),
            v((POOL, RED), F32),
            v((POOL, TAN), F32),
            v((POOL, RED), F32),
            v((2, 8, RED + TAN), F32),
            v((ROWS + 16, RED), BF16),
            v((RED, ROWS), BF16),
            v((RED, 16), BF16),
            v((ROWS + 16, NC), F32),
            v((ROWS, PART), BF16),
            v((ROWS + 16, PART), BF16),
            v((8, PART), F32),
            v((8, PART), F32),
            v((ROWS + 16, RED), F32),
            v((4, 16, RED), F32),
            v((4, 272, RED), BF16),
            v((128, RED), BF16),
            v((144, RED), BF16),
            v((128, RED), BF16),
            v((144, RED), BF16),
            v((272, RED), BF16),
            v((272, RED), BF16),
            v((4, 272, RED), BF16),
            v((RED, 256), BF16),
            v((RED, 16), BF16),
            v((272, RED), BF16),
            v((8, PART), F32),
            v((2, RED, PART), F32),
            v((2, 2, RED, NC), BF16),
            v((2, 2, RED, NC), BF16),
            v((2, 2, 4, 4, 32, NC), BF16),
            v((2, 2, 2, 2, 32, NC), BF16),
            v((2, 2, 2, 2, 32, NC), BF16),
            v((2, 2, 2, 4, 32, NC), BF16),
            v((2, 2, 4, 32, NC), BF16),
            v((2, 2, 4, 32, NC), F32),
            v((2, 2, 3, 32, NC), BF16),
            v((2, 2, 4, 8, NC), BF16),
            v((14, 8, NC), BF16),
            dma((8,)),
            dma((1,)),
            dma((20,)),
            dma((1,)),
            dma((1,)),
            dma((1,)),
            dma((6,)),
            dma((1,)),
            dma((6,)),
            dma((1,)),
            dma((2, 2)),
            dma((1,)),
            dma((2, 2, 3)),
            dma((1,)),
            dma((2, 2)),
            dma((1,)),
            dma((1,)),
        ],
        compiler_params=pltpu.CompilerParams(
            collective_id=0, has_side_effects=True, vmem_limit_bytes=LIMIT
        ),
        name="step",
    )(plan, samples, directions, targets, jacobian_targets, weights)
    return result.astype(F32)[None]


def solution(mesh):
    torus = Mesh(mesh.devices.reshape(4, 4, 2, 2, 2), AXES)
    return jax.shard_map(
        shards,
        mesh=torus,
        in_specs=(
            P(DP, None),
            P(DP, None),
            P(DP, None, None),
            P(DP, None),
            P(DP, None),
            P("zh", None, None),
        ),
        out_specs=P("zh", DP, None),
        check_vma=False,
    )
```

time: 79.6 us -> 71.5 us (0.90)
  Pallas kernels: 77.8 us -> 69.8 us
  local copies, waits for them, and re-layouts: 1.67 us -> 0 us
  other arithmetic: 0 us -> 1.63 us
    pallas_call x1, Pallas kernels: 77.8 us -> 69.8 us  [shards(): pl.pallas_call(kernel, out_shape=jax.ShapeDtypeStruct((8, WIDTH), BF16),...]
    unnamed x1 -> x0, local copies, waits for them, and re-layouts: 1.67 us -> none
    broadcast_in_dim x0 -> x1, other arithmetic: none -> 1.63 us  [shards(): return result.astype(F32)[None]]
where the time goes in v3:
time: 71.5 us; the launch traced here: 71.4 us
  Pallas kernels  69.8 us (98%)
  other arithmetic  1.63 us (2%)
    pallas_call x1, Pallas kernels, shards(): pl.pallas_call(kernel, out_shape=jax.ShapeDtypeStruct((8, WIDTH), BF16),...  69.8 us
    broadcast_in_dim x1, other arithmetic, shards(): return result.astype(F32)[None]  1.63 us

profile of v3, /device:TPU:1, one launch (start us, length us, event | category | flops | bytes accessed | tf_op | source)
XLA Modules:
  0.0 71.4 jit_solution(17728241708298251811)
XLA Ops:
  0.0 69.8 %step.1 = bf16[8,8192]{1,0:T(8,128)(2,1)} custom-call(s32[1,8]{1,0:T(1,128)} %plan_hbm.1, bf16[8,512]{1,0:T(8,128)(2,1)} %samples_hbm.1, s32[8,128]{1,0:T(8,128)} %dirs_hbm.1, bf16[8,512]{1,0:T(8,128)(2,1)} %targets_hbm.1, bf16[8,128,512]{2,1,0:T(8,128)(2,1)} %jt_hbm.1, bf16[1,512,8192]{2,1,0:T(8,128)(2,1)} %w_hbm.1), custom_call_target="tpu_custom_call" | custom-call | tf_op jit(solution)/shard_map/step/pallas_call | solution.py:540
  69.8 1.6 %bitcast_convert_fusion = f32[1,8,8192]{2,1,0:T(8,128)} fusion(bf16[8,8192]{1,0:T(8,128)(2,1)} %step.1), kind=kLoop, calls=%fused_computation | loop fusion | flops 65536 | bytes 393216 | tf_op jit(solution)/shard_map/broadcast_in_dim | solution.py:614

commit v4 on v3

--- a/solution.py
+++ b/solution.py
@@ -82,9 +82,6 @@
     cmb,
     p1r,
     hst,
-    h32,
-    p2r,
-    fs,
     like,
     lsem,
     wss,
@@ -99,8 +96,6 @@
     drs,
     p1s,
     p1q,
-    p2s,
-    p2q,
     p3s,
     p3q,
 ):
@@ -143,9 +138,9 @@
 
     barrier = pltpu.get_barrier_semaphore()
     peers = [n1, n2, dev(pzh=1 - zh)]
-    peers += [dev(pzl=a, pc=1 - c, pzh=b) for a in range(2) for b in range(2)]
     peers += [dev(px=xpeer(o)) for o in (1, 2, 3)]
     peers += [dev(py=ypeer(o)) for o in (1, 2, 3)]
+    peers += [dev(pzl=a, pc=1 - c, pzh=b) for a in (zl, 1 - zl) for b in (zh, 1 - zh)]
     for peer in peers:
         pl.semaphore_signal(barrier, inc=1, device_id=peer, device_id_type=MESH)
 
@@ -157,7 +152,7 @@
     mine = (x, y)
     for k in range(4):
         for kind in range(2):
-            first = pl.multiple_of(PART * (3 - z) + 512 * k + 256 * c + 128 * kind, 128)
+            first = pl.multiple_of(PART * (3 - z) + 1024 * (k // 2) + 512 * c + 256 * (k % 2) + 128 * kind, 128)
             src = w_hbm.at[0, pl.ds(pl.multiple_of(128 * mine[kind], 128), 128), pl.ds(first, 128)]
             pltpu.make_async_copy(src, wst.at[k, kind], lsem.at[6]).start()
     own_w = pltpu.make_async_copy(
@@ -183,7 +178,8 @@
 
     def wslice(layer, core, k, kind, place):
         rows = pl.ds(pl.multiple_of(128 * place, 128), 128)
-        return wb.at[layer, rows, pl.ds(pl.multiple_of(512 * k + 256 * core + 128 * kind, 128), 128)]
+        at = 1024 * (k // 2) + 512 * core + 256 * (k % 2) + 128 * kind
+        return wb.at[layer, rows, pl.ds(pl.multiple_of(at, 128), 128)]
 
     for k in range(4):
         for kind in range(2):
@@ -204,7 +200,7 @@
             for o in (1, 3, 2):
                 to = dev(px=xpeer(o)) if kind == 0 else dev(py=ypeer(o))
                 send(piece, piece, wss.at[0], wrs.at[8 + 2 * k + (o == 2)], to)
-            send(piece, piece, wss.at[0], wrs.at[16 + k], mate)
+            send(piece, piece, wss.at[0], wrs.at[16 + k // 2], mate)
 
     def relay(k):
         for group in ((1, 3), (2,)):
@@ -212,10 +208,13 @@
             for o in group:
                 for kind in range(2):
                     piece = wslice(1 - zh, c, k, kind, lax.rem(mine[kind] + 4 - o, 4))
-                    send(piece, piece, wss.at[0], wrs.at[16 + k], mate)
-
-    def from_mate(k):
-        arrived(wb.at[1 - zh, :, pl.ds(pl.multiple_of(512 * k + 256 * (1 - c), 256), 256)], wrs.at[16 + k])
+                    send(piece, piece, wss.at[0], wrs.at[16 + k // 2], mate)
+
+    def chunk_at(n, core):
+        return pl.multiple_of(1024 * n + 512 * core, NC)
+
+    def from_mate(n):
+        arrived(wb.at[1 - zh, :, pl.ds(chunk_at(n, 1 - c), NC)], wrs.at[16 + n])
 
     from_z(0)
     from_z(1)
@@ -256,22 +255,20 @@
     relay(0)
     from_z(3)
     relay(1)
+    forward(chunk_at(0, c))
+    relay(2)
     from_mate(0)
-    forward(0)
-    relay(2)
+    forward(chunk_at(0, 1 - c))
+    relay(3)
+    forward(chunk_at(1, c))
     from_mate(1)
-    forward(NC)
-    relay(3)
-    from_mate(2)
-    forward(2 * NC)
-    from_mate(3)
 
     own = 2 * zl + zh
     b1 = 2 * (1 - zl) + zh
     b2 = 2 * (1 - zl) + (1 - zh)
     bo = 2 * zl + (1 - zh)
     lo, hi = pl.ds(0, 128), pl.ds(128, 144)
-    cols = pl.ds(3 * NC, NC)
+    cols = pl.ds(chunk_at(1, 1 - c), NC)
     tail16 = slice(ROWS, ROWS + 16)
     slopes(nn(e_buf[tail16, :], wb[0, :, cols])[0:8, :], cols)
     o16 = jac[tail16, :] + nt(tan[tail16, cols], wb[1, :, cols])
@@ -468,6 +465,9 @@
             gst[q, layer] = total.astype(BF16).reshape(4, 4, 32, NC)
             start_unit(q, layer)
 
+    def cols_at(place, q):
+        return pl.ds(pl.multiple_of(HALF * place + NC * q, NC), NC)
+
     for q in range(2):
         for layer in (1, 0):
             forward_unit(q, layer)
@@ -479,58 +479,38 @@
                 total = g[layer, rows_for(layer, x if layer == 1 else y, k), cols]
                 for side in range(2):
                     total = total + p1r[q, layer, side, k].astype(F32)
-                hst[q, layer, k] = total.astype(BF16)
-                h32[q, layer, k] = total
-            for o in (2, 1, 3):
-                if layer == 1:
-                    src, to = hst.at[q, layer, ypeer(o)], dev(py=ypeer(o))
-                else:
-                    src, to = hst.at[q, layer, xpeer(o)], dev(px=xpeer(o))
-                send(
-                    src,
-                    p2r.at[q, layer, o - 1],
-                    p2s.at[0],
-                    p2q.at[q, layer],
-                    to,
-                )
-
-    others = [(a, b, d) for a in (1, 0) for b in (1, 0) for d in (1, 0) if a + b + d]
-
-    def moved(step):
-        pzh, pzl, pc = (lax.rem(a + b, 2) for a, b in zip((zh, zl, c), step))
-        return pzh, pzl, pc
-
-    def out_at(pzh, pzl, pc, q):
-        return pl.ds(pl.multiple_of(PART * (2 * pzh + pzl) + HALF * pc + NC * q, NC), NC)
-
-    for q in range(2):
-        for layer in (1, 0):
-            arrived(p2r.at[q, layer], p2q.at[q, layer])
-            total = h32[q, layer, y if layer == 1 else x]
-            for o in (1, 3, 2):
-                total = total + p2r[q, layer, o - 1].astype(F32)
-            for k in range(4):
-                fs[q, layer, k] = total[8 * k : 8 * k + 8, :].astype(BF16)
-        for step in others:
-            pzh, pzl, pc = moved(step)
-            send(
-                fs.at[q, pzh, 2 * pzl + pc],
-                out.at[:, out_at(zh, zl, c, q)],
-                p3s.at[0],
-                p3q.at[0],
-                dev(pzl=pzl, pc=pc, pzh=pzh),
-            )
-        pltpu.make_async_copy(fs.at[q, zh, 2 * zl + c], out.at[:, out_at(zh, zl, c, q)], lsem.at[7]).start()
+                for part in range(4):
+                    hst[q, layer, k, part] = total[8 * part : 8 * part + 8, :].astype(BF16)
+            ring = y if layer == 1 else x
+            slot = out.at[ring, :, cols_at(2 * z + c, q)]
+            for o in (2, 1, 3, 0):
+                place = lax.rem(ring + o, 4)
+                for a, b in ((1, 1), (1, 0), (0, 1), (0, 0)):
+                    pzl, pc = lax.rem(zl + a, 2), lax.rem(c + b, 2)
+                    src = hst.at[q, layer, place, 2 * pzl + pc]
+                    to = dev(pzl=pzl, pc=pc, pzh=layer)
+                    to = (to[0], place, *to[2:]) if layer == 1 else (place, *to[1:])
+                    if o + a + b:
+                        send(src, slot, p3s.at[0], p3q.at[0], to)
+                        continue
+
+                    @pl.when(zh != layer)
+                    def _():
+                        send(src, slot, p3s.at[0], p3q.at[0], to)
+
+                    @pl.when(zh == layer)
+                    def _():
+                        pltpu.make_async_copy(src, slot, lsem.at[7]).start()
+
     arrived(like, p3q.at[0])
-    pltpu.make_async_copy(fs.at[0, 0, pl.ds(0, 2)], fs.at[0, 0, pl.ds(0, 2)], lsem.at[7]).wait()
     sent(wb.at[0], wss.at[0])
     sent(xd.at[0], xss.at[0])
     sent(sa.at[pl.ds(0, 3)], rss.at[0])
     sent(mb.at[pl.ds(0, 3)], ass_.at[0])
     sent(ds, dss.at[0])
     sent(gst.at[:, :, pl.ds(0, 3)], p1s.at[0])
-    sent(p2r, p2s.at[0])
     sent(like, p3s.at[0])
+    pltpu.make_async_copy(like.at[0:2], like.at[0:2], lsem.at[7]).wait()
 
 
 def shards(samples, targets, jacobian_targets, directions, plan, weights):
@@ -539,7 +519,7 @@
     v = pltpu.VMEM
     result = pl.pallas_call(
         kernel,
-        out_shape=jax.ShapeDtypeStruct((8, WIDTH), BF16),
+        out_shape=jax.ShapeDtypeStruct((4, 8, WIDTH), BF16),
         in_specs=[anywhere] * 6,
         out_specs=anywhere,
         scratch_shapes=[
@@ -583,14 +563,11 @@
             v((2, 2, 2, 2, 32, NC), BF16),
             v((2, 2, 2, 2, 32, NC), BF16),
             v((2, 2, 2, 4, 32, NC), BF16),
-            v((2, 2, 4, 32, NC), BF16),
-            v((2, 2, 4, 32, NC), F32),
-            v((2, 2, 3, 32, NC), BF16),
-            v((2, 2, 4, 8, NC), BF16),
-            v((14, 8, NC), BF16),
+            v((2, 2, 4, 4, 8, NC), BF16),
+            v((62, 8, NC), BF16),
             dma((8,)),
             dma((1,)),
-            dma((20,)),
+            dma((18,)),
             dma((1,)),
             dma((1,)),
             dma((1,)),
@@ -601,8 +578,6 @@
             dma((2, 2)),
             dma((1,)),
             dma((2, 2, 3)),
-            dma((1,)),
-            dma((2, 2)),
             dma((1,)),
             dma((1,)),
         ],
@@ -611,7 +586,7 @@
         ),
         name="step",
     )(plan, samples, directions, targets, jacobian_targets, weights)
-    return result.astype(F32)[None]
+    return sum(result[k].astype(F32) for k in range(4))[None]
 
 
 def solution(mesh):

time: 71.5 us -> 69.3 us (0.969)
  Pallas kernels: 69.8 us -> 67.3 us
    pallas_call x1, Pallas kernels: 69.8 us -> 67.3 us  [shards(): pl.pallas_call(kernel, out_shape=jax.ShapeDtypeStruct((4, 8, WIDTH), BF16...]
    add x0 -> x1, other arithmetic: none -> 1.86 us  [shards(): return sum((result[k].astype(F32) for k in range(4)))[None]]
    broadcast_in_dim x1 -> x0, other arithmetic: 1.63 us -> none  [shards(): return result.astype(F32)[None]]
where the time goes in v4:
time: 69.3 us; the launch traced here: 69.2 us
  Pallas kernels  67.3 us (97%)
  other arithmetic  1.86 us (3%)
    pallas_call x1, Pallas kernels, shards(): pl.pallas_call(kernel, out_shape=jax.ShapeDtypeStruct((4, 8, WIDTH), BF16...  67.3 us
    add x1, other arithmetic, shards(): return sum((result[k].astype(F32) for k in range(4)))[None]  1.86 us

profile of v4, /device:TPU:1, one launch (start us, length us, event | category | flops | bytes accessed | tf_op | source)
XLA Modules:
  0.0 69.2 jit_solution(4904208366963642561)
XLA Ops:
  0.0 67.3 %step.1 = bf16[4,8,8192]{2,1,0:T(8,128)(2,1)} custom-call(s32[1,8]{1,0:T(1,128)} %plan_hbm.1, bf16[8,512]{1,0:T(8,128)(2,1)} %samples_hbm.1, s32[8,128]{1,0:T(8,128)} %dirs_hbm.1, bf16[8,512]{1,0:T(8,128)(2,1)} %targets_hbm.1, bf16[8,128,512]{2,1,0:T(8,128)(2,1)} %jt_hbm.1, bf16[1,512,8192]{2,1,0:T(8,128)(2,1)} %w_hbm.1), custom_call_target="tpu_custom_call" | custom-call | tf_op jit(solution)/shard_map/step/pallas_call | solution.py:520
  67.4 1.9 %convert_add_fusion = f32[1,8,8192]{2,1,0:T(8,128)} fusion(bf16[4,8,8192]{2,1,0:T(8,128)(2,1)} %step.1), kind=kLoop, calls=%fused_computation | loop fusion | flops 458752 | bytes 786432 | tf_op jit(solution)/shard_map/add | solution.py:589

commit v5 on v4

--- a/solution.py
+++ b/solution.py
@@ -242,14 +242,17 @@
 
     def forward(start):
         cols = pl.ds(pl.multiple_of(start, NC), NC)
-        p32[...] = nn(e_buf[...], wb[0, :, cols])
+        halves = ((512, ROWS + 16), (0, 512))
+        for low, high in halves:
+            p32[low:high, :] = nn(e_buf[low:high, :], wb[0, :, cols])
         slope = slopes(p32[ROWS : ROWS + 8, :], cols)
-        for j in range(8):
-            rows = slice(TAN * j, TAN * (j + 1))
-            picked = p32[rows, :]
-            pk[rows, cols] = picked.astype(BF16)
-            tan[rows, cols] = (slope[j : j + 1, :] * picked).astype(BF16)
-        jac[...] += nt(tan[:, cols], wb[1, :, cols])
+        for low, high in halves:
+            for j in range(low // TAN, low // TAN + 4):
+                rows = slice(TAN * j, TAN * (j + 1))
+                picked = p32[rows, :]
+                pk[rows, cols] = picked.astype(BF16)
+                tan[rows, cols] = (slope[j : j + 1, :] * picked).astype(BF16)
+            jac[low:high, :] += nt(tan[low:high, cols], wb[1, :, cols])
 
     from_z(2)
     relay(0)
@@ -270,21 +273,28 @@
     lo, hi = pl.ds(0, 128), pl.ds(128, 144)
     cols = pl.ds(chunk_at(1, 1 - c), NC)
     tail16 = slice(ROWS, ROWS + 16)
-    slopes(nn(e_buf[tail16, :], wb[0, :, cols])[0:8, :], cols)
-    o16 = jac[tail16, :] + nt(tan[tail16, cols], wb[1, :, cols])
-    for b in range(4):
-        o2 = jnp.concatenate([o16[2 * b : 2 * b + 2, :], jnp.zeros((14, RED), F32)], axis=0)
-        ox[b] = o2
-        sa[b, 256:272, :] = o2.astype(BF16)
     for b, kind in ((bo, 0), (b1, 1), (b2, 2), (own, 3)):
         rows = pl.ds(pl.multiple_of(256 * b, 256), 256)
-        p32[0:256, :] = nn(e_buf[rows, :], wb[0, :, cols])
+        if kind == 0:
+            p32[0:272, :] = nn(jnp.concatenate([e_buf[rows, :], e_buf[tail16, :]], axis=0), wb[0, :, cols])
+            slopes(p32[256:264, :], cols)
+        else:
+            p32[0:256, :] = nn(e_buf[rows, :], wb[0, :, cols])
         for e in range(2):
             half = pl.ds(pl.multiple_of(256 * b + 128 * e, 128), 128)
             picked = p32[128 * e : 128 * e + 128, :]
             pk[half, cols] = picked.astype(BF16)
             tan[half, cols] = (s1[pl.ds(2 * b + e, 1), cols] * picked).astype(BF16)
-        done = jac[rows, :] + nt(tan[rows, cols], wb[1, :, cols])
+        if kind == 0:
+            both = nt(jnp.concatenate([tan[rows, cols], tan[tail16, cols]], axis=0), wb[1, :, cols])
+            done = jac[rows, :] + both[0:256, :]
+            o16 = jac[tail16, :] + both[256:272, :]
+            for k in range(4):
+                o2 = jnp.concatenate([o16[2 * k : 2 * k + 2, :], jnp.zeros((14, RED), F32)], axis=0)
+                ox[k] = o2
+                sa[k, 256:272, :] = o2.astype(BF16)
+        else:
+            done = jac[rows, :] + nt(tan[rows, cols], wb[1, :, cols])
         if kind == 3:
             jac[rows, :] = done
         else:
@@ -401,7 +411,7 @@
         at = 128 * place + 32 * k if layer == 1 else 128 * k + 32 * place
         return pl.ds(pl.multiple_of(at, 32), 32)
 
-    def start_unit(q, layer):
+    def start_unit(q, layer, steps):
         across = xpeer(2) if layer == 1 else ypeer(2)
         up, down = ahead(layer), behind(layer)
         moves = (
@@ -410,7 +420,8 @@
             (half_for(q, layer, up, 1), p1r.at[q, layer, 0, pl.ds(2, 2)], up),
             (half_for(q, layer, down, 0), p1r.at[q, layer, 1, pl.ds(0, 2)], down),
         )
-        for k, (src, dst, place) in enumerate(moves):
+        for k in steps:
+            src, dst, place = moves[k]
             send(src, dst, p1s.at[0], p1q.at[q, layer, min(k, 2)], at_place(layer, place))
 
     def forward_unit(q, layer):
@@ -463,14 +474,16 @@
             total = g[layer, :, cols] + dr[q, layer].astype(F32)
             g[layer, :, cols] = total
             gst[q, layer] = total.astype(BF16).reshape(4, 4, 32, NC)
-            start_unit(q, layer)
+            start_unit(q, layer, range(4) if q == 0 else range(2))
 
     def cols_at(place, q):
         return pl.ds(pl.multiple_of(HALF * place + NC * q, NC), NC)
 
-    for q in range(2):
-        for layer in (1, 0):
-            forward_unit(q, layer)
+    for layer in (1, 0):
+        forward_unit(0, layer)
+        start_unit(1, layer, range(2, 4))
+    for layer in (1, 0):
+        forward_unit(1, layer)
     for q in range(2):
         cols = pl.ds(pl.multiple_of(HALF * c + NC * q, NC), NC)
         for layer in (1, 0):

time: 69.3 us -> 68.9 us (level)
  no operation moved by 1% of the time
where the time goes in v5:
time: 68.9 us; the launch traced here: 68.8 us
  Pallas kernels  66.9 us (97%)
  other arithmetic  1.86 us (3%)
    pallas_call x1, Pallas kernels, shards(): pl.pallas_call(kernel, out_shape=jax.ShapeDtypeStruct((4, 8, WIDTH), BF16...  66.9 us
    add x1, other arithmetic, shards(): return sum((result[k].astype(F32) for k in range(4)))[None]  1.86 us

profile of v5, /device:TPU:1, one launch (start us, length us, event | category | flops | bytes accessed | tf_op | source)
XLA Modules:
  0.0 68.8 jit_solution(14596684192875844920)
XLA Ops:
  0.0 66.9 %step.1 = bf16[4,8,8192]{2,1,0:T(8,128)(2,1)} custom-call(s32[1,8]{1,0:T(1,128)} %plan_hbm.1, bf16[8,512]{1,0:T(8,128)(2,1)} %samples_hbm.1, s32[8,128]{1,0:T(8,128)} %dirs_hbm.1, bf16[8,512]{1,0:T(8,128)(2,1)} %targets_hbm.1, bf16[8,128,512]{2,1,0:T(8,128)(2,1)} %jt_hbm.1, bf16[1,512,8192]{2,1,0:T(8,128)(2,1)} %w_hbm.1), custom_call_target="tpu_custom_call" | custom-call | tf_op jit(solution)/shard_map/step/pallas_call | solution.py:533
  66.9 1.9 %convert_add_fusion = f32[1,8,8192]{2,1,0:T(8,128)} fusion(bf16[4,8,8192]{2,1,0:T(8,128)(2,1)} %step.1), kind=kLoop, calls=%fused_computation | loop fusion | flops 458752 | bytes 786432 | tf_op jit(solution)/shard_map/add | solution.py:602

commit v6 on v5

--- a/solution.py
+++ b/solution.py
@@ -337,8 +337,10 @@
     def ends(pair):
         return [(b, 128 * e, pl.ds(pl.multiple_of(256 * b + 128 * e, 128), 128), 2 * b + e) for b, e in pair]
 
-    def turn(pair):
+    def turn(pair, some=(0, 1)):
         for k, (b, at, _, _) in enumerate(ends(pair)):
+            if k not in some:
+                continue
             mt[:, 128 * k : 128 * k + 128] = jnp.transpose(mb[b, at : at + 128, :])
             lm[128 * k : 128 * k + 128, :] = mb[b, at : at + 128, :]
 
@@ -383,11 +385,12 @@
     arrived(mb.at[b2, lo], ars.at[1])
     arrived(mb.at[b1, hi], ars.at[2])
     backward(((b1, 1), (b2, 0)), False)
+    tail = ((bo, 0), (bo, 1))
     arrived(mb.at[bo, lo], ars.at[4])
+    turn(tail, (0,))
     arrived(mb.at[bo, hi], ars.at[5])
-
-    tail = ((bo, 0), (bo, 1))
-    turn(tail)
+    turn(tail, (1,))
+
     heads = [mb[b, 256:272, :].astype(F32)[0:2, :] for b in range(4)]
     m16 = jnp.concatenate(heads + [jnp.zeros((8, RED), F32)], axis=0)
     lm[256:272, :] = m16.astype(BF16)

time: 68.9 us -> 69 us (level)
  no operation moved by 1% of the time
where the time goes in v6:
time: 69 us; the launch traced here: 68.8 us
  Pallas kernels  67 us (97%)
  other arithmetic  1.86 us (3%)
    pallas_call x1, Pallas kernels, shards(): pl.pallas_call(kernel, out_shape=jax.ShapeDtypeStruct((4, 8, WIDTH), BF16...  67 us
    add x1, other arithmetic, shards(): return sum((result[k].astype(F32) for k in range(4)))[None]  1.86 us

profile of v6, /device:TPU:1, one launch (start us, length us, event | category | flops | bytes accessed | tf_op | source)
XLA Modules:
  0.0 68.8 jit_solution(6086987750832859965)
XLA Ops:
  0.0 67.0 %step.1 = bf16[4,8,8192]{2,1,0:T(8,128)(2,1)} custom-call(s32[1,8]{1,0:T(1,128)} %plan_hbm.1, bf16[8,512]{1,0:T(8,128)(2,1)} %samples_hbm.1, s32[8,128]{1,0:T(8,128)} %dirs_hbm.1, bf16[8,512]{1,0:T(8,128)(2,1)} %targets_hbm.1, bf16[8,128,512]{2,1,0:T(8,128)(2,1)} %jt_hbm.1, bf16[1,512,8192]{2,1,0:T(8,128)(2,1)} %w_hbm.1), custom_call_target="tpu_custom_call" | custom-call | tf_op jit(solution)/shard_map/step/pallas_call | solution.py:536
  67.0 1.9 %convert_add_fusion = f32[1,8,8192]{2,1,0:T(8,128)} fusion(bf16[4,8,8192]{2,1,0:T(8,128)(2,1)} %step.1), kind=kLoop, calls=%fused_computation | loop fusion | flops 458752 | bytes 786432 | tf_op jit(solution)/shard_map/add | solution.py:605
